TPU v7x, 256 devices: a whole 4x4x8 slice. The times are simulated.
256 devices in a mesh: dp: 64 (over z, y, core), vocab: 4 (over x).
Axes of the slice: x: 4, y: 4, z: 8, core: 2. Of those that a mesh axis runs over, the one named last changes fastest.
Arguments:
- hidden_in: bfloat16 [512, 24, 1024], P(('dp', 'vocab')), may hold values from -6 to 6
- tokens: int32 [512, 24], P(('dp', 'vocab')), may hold values from 0 to 131071
- lengths: int32 [512], P(('dp', 'vocab')), may hold values from 2 to 24, as said below
- cutoff: int32 [1], replicated, may hold values from 1 to 512
- norm_gain: float32 [1024], replicated, may hold values from 0.5 to 1.5
- gate_weight: bfloat16 [1024, 4096], P(None, 'vocab'), may hold values from -0.1875 to 0.1875
- up_weight: bfloat16 [1024, 4096], P(None, 'vocab'), may hold values from -0.1875 to 0.1875
- down_weight: bfloat16 [4096, 1024], P('vocab'), may hold values from -0.09375 to 0.09375
- final_gain: float32 [1024], replicated, may hold values from 0.5 to 1.5
- head_table: bfloat16 [131072, 1024], P(('dp', 'vocab')), may hold values from -12 to 12
Outputs:
- log_ppl: float32 [512], P(('dp', 'vocab'))
- margin: float32 [512], P(('dp', 'vocab'))
Inputs may be any that keep to these rules, and one draw needn't show every extreme that they name: Every length is 2 or more; the documents of one device have together at most 32 positions below their lengths, and some device has exactly 32.
All inputs are finite; a program needn't handle non-finite values.
Results may differ from a plain program's by a relative error of at most 0.025.
Values may be sent and summed in bfloat16 or wider, within the bound.
No kernel may reach another device: no remote copies, remote signals or barrier semaphores. Data moves between devices by JAX's collectives and lax.ppermute only.
A program may use at most 64 MiB of HBM per device.

v0:
```python
import jax
import jax.numpy as jnp
from jax import lax
from jax.experimental import pallas as pl
from jax.experimental.pallas import tpu as pltpu
from jax.sharding import Mesh
from jax.sharding import PartitionSpec as P

CAP = 32
EXTRA = 8
LANES = 4 * CAP
TILE = 256
AXES = ("z", "y", "c", "x")
X_STEPS = (0, -1, 2, 1)
HIGHEST = lax.Precision.HIGHEST
F32 = jnp.float32
BF16 = jnp.bfloat16
VMEM = pl.BlockSpec(memory_space=pltpu.VMEM)
SMEM = pl.BlockSpec(memory_space=pltpu.SMEM)


def params(mib):
    return pltpu.CompilerParams(vmem_limit_bytes=mib * 1024 * 1024)


def cost(flops, moved=0, exps=0):
    return pl.CostEstimate(flops=flops, bytes_accessed=moved, transcendentals=exps)


def shift(array, axis, step):
    length = lax.axis_size(axis)
    pairs = [(i, (i + step) % length) for i in range(length)]
    return lax.ppermute(array, axis, pairs)


def rms_norm(values, gain):
    squares = jnp.mean(values * values, axis=-1, keepdims=True)
    return values * lax.rsqrt(squares + 1e-06) * gain


def iota(shape, dim):
    return lax.broadcasted_iota(jnp.int32, shape, dim)


def prepare_kernel(lengths_ref, tokens_ref, hidden_ref, gain_ref, sent_ref, residual_ref):
    docs, length, width = hidden_ref.shape
    lives = [lengths_ref[d] - 1 for d in range(docs)]
    starts = [0, lives[0]]
    residual = jnp.zeros((CAP, width), F32)
    target = jnp.zeros((8, CAP), F32)
    slot_down, place_right = iota((CAP, length), 0), iota((CAP, length), 1)
    place_down, slot_right = iota((length, CAP), 0), iota((length, CAP), 1)
    for d in range(docs):
        live = (slot_down >= starts[d]) & (slot_down < starts[d] + lives[d])
        placing = (place_right == slot_down - starts[d]) & live
        residual = residual + jnp.dot(
            placing.astype(BF16), hidden_ref[d], preferred_element_type=F32
        )
        live = (slot_right >= starts[d]) & (slot_right < starts[d] + lives[d])
        taking = (place_down == slot_right - starts[d] + 1) & live
        token = tokens_ref[d : d + 1, :]
        digits = [token & 255, (token >> 8) & 255, token >> 16]
        digits = jnp.concatenate(digits + [jnp.zeros((5, length), jnp.int32)], axis=0)
        target = target + jnp.dot(
            digits.astype(F32).astype(BF16), taking.astype(BF16), preferred_element_type=F32
        )
    residual_ref[...] = residual.astype(BF16)
    sent_ref[:CAP, :] = rms_norm(residual, gain_ref[...]).astype(BF16)
    row, slot = iota((8, CAP), 0), iota((8, CAP), 1)
    for d in range(docs):
        live = (slot >= starts[d]) & (slot < starts[d] + lives[d]) & (row == 3 + d)
        target = jnp.where(live, lives[d].astype(F32), target)
    sent_ref[CAP:, :] = jnp.concatenate([target, jnp.zeros((8, width - CAP), F32)], axis=1).astype(
        BF16
    )


def feed_kernel(*refs):
    arrived, (gate_ref, up_ref, down_ref) = refs[:4], refs[4:7]
    own_ref, out_refs, meta_ref, rows = refs[7], refs[8:11], refs[11], refs[12]
    for k, ref in enumerate(arrived):
        rows[k * CAP : (k + 1) * CAP, :] = ref[:CAP, :]
    metas = jnp.concatenate([ref[CAP:, :CAP].astype(F32) for ref in arrived], axis=1)
    meta_ref[...] = jnp.zeros_like(meta_ref)
    meta_ref[:, :LANES] = metas.astype(BF16)
    segment = rows[...]
    units = gate_ref.shape[1]
    total = jnp.zeros((4 * CAP, down_ref.shape[1]), F32)
    for at in range(0, units, 2 * TILE):
        span = slice(at, at + 2 * TILE)
        gate = jnp.dot(segment, gate_ref[:, span], preferred_element_type=F32)
        up = jnp.dot(segment, up_ref[:, span], preferred_element_type=F32)
        active = (gate / (1.0 + jnp.exp(-gate)) * up).astype(BF16)
        total = total + jnp.dot(active, down_ref[span, :], preferred_element_type=F32)
    own_ref[...] = total[:CAP]
    for k, ref in enumerate(out_refs):
        ref[...] = total[(k + 1) * CAP : (k + 2) * CAP].astype(BF16)


def finish_kernel(own_ref, first_ref, second_ref, third_ref, residual_ref, gain_ref, out_ref):
    branch = own_ref[...] + first_ref[...].astype(F32)
    branch = branch + second_ref[...].astype(F32) + third_ref[...].astype(F32)
    stream = (residual_ref[...].astype(F32) + branch).astype(BF16)
    out_ref[...] = rms_norm(stream.astype(F32), gain_ref[...]).astype(BF16)


def join_kernel(*refs):
    out_ref, at = refs[-1], 0
    for ref in refs[:-1]:
        out_ref[at : at + ref.shape[0], :] = ref[...]
        at += ref.shape[0]


def stage_kernel(*refs):
    count = (len(refs) - 1) // 2
    copies = [
        pltpu.make_async_copy(refs[k], refs[count + k], refs[-1].at[k]) for k in range(count)
    ]
    for copy in copies:
        copy.start()
    for copy in copies:
        copy.wait()


def score_kernel(layout, table_steps, *refs):
    chunk_count, held = len(layout), sum(layout)
    chunk_refs, refs = list(refs[:held]), refs[held:]
    table_refs, (out_ref, rows, targets, results) = refs[:-4], refs[-4:]
    metas = []
    for k, parts in enumerate(layout):
        metas.append(chunk_refs[0][LANES:, :LANES].astype(F32))
        span = rows.shape[1] // parts
        for part in range(parts):
            rows[k * LANES : (k + 1) * LANES, part * span : (part + 1) * span] = chunk_refs.pop(0)[
                :LANES, :
            ]
    groups, total = chunk_count // 2, 2 * LANES
    for k, meta in enumerate(metas):
        target = meta[0:1] + 256.0 * meta[1:2] + 65536.0 * meta[2:3]
        targets[k // 2, :, (k % 2) * LANES : (k % 2 + 1) * LANES] = target.astype(jnp.int32)
    column = iota((TILE, total), 0)
    z, y, c, x = [lax.axis_index(axis) for axis in AXES]

    def score_group(group, carry):
        left = rows[pl.ds(pl.multiple_of(group * total, total), total), :]
        target = targets[group]
        peak = jnp.full((8, total), -3.0e38, F32)
        exp_sum = jnp.zeros((8, total), F32)
        picked = jnp.zeros((8, total), F32)
        for table, (y_steps, c_step) in zip(table_refs, table_steps):
            for tile in range(table.shape[0] // TILE):
                y_at, c_at = lax.rem(y + y_steps[tile // 2], 4), lax.rem(c + c_step, 2)
                shard_at = ((z * 4 + y_at) * 2 + c_at) * 4 + x
                local = target - (2 * shard_at + tile % 2) * TILE
                logits = lax.dot_general(
                    table[tile * TILE : (tile + 1) * TILE, :],
                    left,
                    (((1,), (1,)), ((), ())),
                    preferred_element_type=F32,
                )
                found = jnp.where(column == local, logits, 0.0)
                grouped = logits.reshape(TILE // 8, 8, total)
                highest = jnp.maximum(peak, jnp.max(grouped, axis=0))
                exp_sum = exp_sum * jnp.exp(peak - highest) + jnp.sum(
                    jnp.exp(grouped - highest[None]), axis=0
                )
                picked = picked + jnp.sum(found.reshape(TILE // 8, 8, total), axis=0)
                peak = highest
        top = jnp.max(peak, axis=0, keepdims=True)
        lse = top + jnp.log(jnp.sum(exp_sum * jnp.exp(peak - top), axis=0, keepdims=True))
        results[group, 0:1, :] = lse
        results[group, 1:2, :] = jnp.sum(picked, axis=0, keepdims=True)
        return carry

    if groups == 1:
        score_group(0, 0)
    else:
        lax.fori_loop(0, groups, score_group, 0)
    for k, meta in enumerate(metas):
        part = slice((k % 2) * LANES, (k % 2 + 1) * LANES)
        lse, pick = results[k // 2, 0:1, part], results[k // 2, 1:2, part]
        first, second = [
            jnp.where(line > 0.0, 1.0 / jnp.maximum(line, 1.0), 0.0)
            for line in (meta[3:4], meta[4:5])
        ]
        lines = [lse, first * pick, second * pick, first, second]
        out_ref[k] = jnp.concatenate(lines + [jnp.zeros((3, LANES), F32)], axis=0)


def document_sums(first, second):
    slot_at, lane_at = iota((LANES, LANES), 0), iota((LANES, LANES), 1)
    same = slot_at // CAP == lane_at // CAP
    sums = jnp.zeros_like(first)
    for values, lane in ((first, CAP - 2), (second, CAP - 1)):
        into = (same & (lane_at % CAP == lane)).astype(F32)
        sums = sums + jnp.dot(values, into, precision=HIGHEST, preferred_element_type=F32)
    return sums


def message_kernel(near_ref, middle_ref, far_ref, outer_ref, last_ref, out_ref, weight_ref):
    def joined(left, right):
        top = jnp.maximum(left[0:1], right[0:1])
        lse = top + jnp.log(jnp.exp(left[0:1] - top) + jnp.exp(right[0:1] - top))
        return jnp.concatenate([lse, left[1:3] + right[1:3], left[3:]], axis=0)

    near = [joined(near_ref[k], far_ref[k]) for k in range(2)]
    middle = [joined(middle_ref[k], far_ref[2 + k]) for k in range(2)]
    order = [
        last_ref[0],
        near[1],
        middle[1],
        outer_ref[1],
        last_ref[1],
        outer_ref[0],
        middle[0],
        near[0],
    ]
    kinds = [jnp.concatenate([part[k : k + 1] for part in order], axis=0) for k in range(5)]
    kinds = [
        pltpu.roll(pltpu.roll(kind, lax.axis_index("z"), 0), lax.axis_index("x") * CAP, 1)
        for kind in kinds
    ]
    lse, pick_first, pick_second, weight_first, weight_second = kinds
    weight_ref[0] = weight_first
    weight_ref[1] = weight_second
    carried = iota((8, LANES), 1) % CAP >= CAP - 2
    message = jnp.where(carried, document_sums(pick_first, pick_second), lse)
    for k in range(out_ref.shape[0]):
        out_ref[k] = message


def merge_kernel(everyone_ref, weight_ref, out_ref):
    members = everyone_ref.shape[0]
    top = everyone_ref[0]
    total = everyone_ref[0]
    for k in range(1, members):
        top = jnp.maximum(top, everyone_ref[k])
        total = total + everyone_ref[k]
    exp_sum = jnp.zeros_like(top)
    for k in range(members):
        exp_sum = exp_sum + jnp.exp(everyone_ref[k] - top)
    lse = top + jnp.log(exp_sum)
    carried = iota((8, LANES), 1) % CAP >= CAP - 2
    lse = jnp.where(carried, 0.0, lse)
    sums = document_sums(weight_ref[0] * lse, weight_ref[1] * lse)
    group = jnp.where(carried, sums - total, 0.0)
    for k in range(out_ref.shape[0]):
        out_ref[k] = group


def select_kernel(cutoff_ref, groups_ref, log_ref, margin_ref):
    values = groups_ref[...].reshape(-1, LANES)
    across = values.T
    count = values.shape[0]
    lanes = [x * CAP + CAP - 2 + d for x in range(4) for d in range(2)]
    best = jnp.full((count, 1), jnp.inf, F32)
    for lane in lanes:
        value = values[:, lane : lane + 1]
        below = jnp.zeros((count, count), F32)
        for other in lanes:
            below = below + jnp.where(across[other : other + 1, :] <= value, 1.0, 0.0)
        rank = jnp.sum(below, axis=1, keepdims=True)
        best = jnp.minimum(
            best, jnp.where(rank >= cutoff_ref[0].astype(F32), value, jnp.inf)
        )
    threshold = jnp.min(best)
    own = groups_ref[lax.axis_index("y") * 2 + lax.axis_index("c")]
    row, lane_at = iota((8, LANES), 0), iota((8, LANES), 1)
    for d in range(2):
        here = (row == lax.axis_index("z")) & (
            lane_at == lax.axis_index("x") * CAP + CAP - 2 + d
        )
        log_ppl = jnp.sum(jnp.where(here, own, 0.0))
        log_ref[d] = log_ppl
        margin_ref[d] = log_ppl - threshold


def on_device(
    hidden_in,
    tokens,
    lengths,
    cutoff,
    norm_gain,
    gate_weight,
    up_weight,
    down_weight,
    final_gain,
    head_table,
):
    width = hidden_in.shape[2]
    shard = head_table.shape[0]
    half_shard, half = shard // 2, width // 2
    size = {axis: lax.axis_size(axis) for axis in AXES}

    sent, residual = pl.pallas_call(
        prepare_kernel,
        out_shape=(pltpu.VMEM((CAP + EXTRA, width), BF16), pltpu.VMEM((CAP, width), BF16)),
        in_specs=[SMEM, VMEM, VMEM, VMEM],
        out_specs=(VMEM, VMEM),
        cost_estimate=cost(4_000_000),
        compiler_params=params(58),
    )(lengths, tokens, hidden_in, norm_gain.reshape(1, width))
    arrived = [sent if step == 0 else shift(sent, "x", step) for step in X_STEPS]

    weights = (gate_weight, up_weight, down_weight)
    *weights, _ = lax.optimization_barrier((*weights, sent))
    weights = pl.pallas_call(
        stage_kernel,
        out_shape=tuple(pltpu.VMEM(weight.shape, BF16) for weight in weights),
        in_specs=[pl.BlockSpec(memory_space=pltpu.HBM)] * 3,
        out_specs=(VMEM,) * 3,
        scratch_shapes=[pltpu.SemaphoreType.DMA((3,))],
        cost_estimate=cost(3_000_000, 6_300_000),
        compiler_params=params(54),
    )(*weights)
    from_below = shift(head_table, "y", 1)
    from_above = shift(head_table, "y", -1)
    partials = pl.pallas_call(
        feed_kernel,
        out_shape=(
            jax.ShapeDtypeStruct((CAP, width), F32),
            *(jax.ShapeDtypeStruct((CAP, width), BF16),) * 3,
            jax.ShapeDtypeStruct((EXTRA, width), BF16),
        ),
        in_specs=[VMEM] * 7,
        out_specs=(VMEM,) * 5,
        scratch_shapes=[pltpu.VMEM((4 * CAP, width), BF16)],
        cost_estimate=cost(800_000_000, 6_300_000, 131072),
        compiler_params=params(16),
    )(*arrived, *weights)
    own_part, parts, meta = partials[0], partials[1:4], partials[4]
    returned = [shift(part, "x", -step) for part, step in zip(parts, X_STEPS[1:])]
    final_rows = pl.pallas_call(
        finish_kernel,
        out_shape=jax.ShapeDtypeStruct((CAP, width), BF16),
        in_specs=[VMEM] * 6,
        out_specs=VMEM,
        cost_estimate=cost(1_000_000),
        compiler_params=params(4),
    )(own_part, *returned, residual, final_gain.reshape(1, width))


    def joined(parts):
        rows = sum(part.shape[0] for part in parts)
        return pl.pallas_call(
            join_kernel,
            out_shape=jax.ShapeDtypeStruct((rows, width), BF16),
            in_specs=[VMEM] * len(parts),
            out_specs=VMEM,
            cost_estimate=cost(500_000),
            compiler_params=params(4),
        )(*parts)

    chunk = joined([final_rows if s == 0 else shift(final_rows, "x", s) for s in X_STEPS] + [meta])

    def step_on(below, above):
        return shift(below, "z", 1), shift(above, "z", -1)

    up_1, down_1 = step_on(chunk, chunk)
    chunk, from_below, from_above = lax.optimization_barrier((chunk, from_below, from_above))
    far = [shift(from_below[:half_shard], "y", 1), shift(from_above[half_shard:], "y", -1)]
    near_table = joined([head_table, from_below, from_above])
    near_tables = [near_table, shift(near_table, "c", 1)]
    near_steps = [((0, 3, 1), 0), ((0, 3, 1), 1)]
    far_steps = [((2,), 0), ((2,), 1)]

    def score(chunks, tables, table_steps):
        rows = len(chunks) * LANES
        entries = sum(table.shape[0] for table in tables)
        refs = [part for chunk in chunks for part in chunk]
        layout = [len(chunk) for chunk in chunks]

        def kernel(*refs):
            score_kernel(layout, table_steps, *refs)

        return pl.pallas_call(
            kernel,
            out_shape=jax.ShapeDtypeStruct((len(chunks), 8, LANES), F32),
            in_specs=[VMEM] * (len(refs) + len(tables)),
            out_specs=VMEM,
            scratch_shapes=[
                pltpu.VMEM((rows, width), BF16),
                pltpu.VMEM((len(chunks) // 2, 1, 2 * LANES), jnp.int32),
                pltpu.VMEM((len(chunks) // 2, 8, 2 * LANES), F32),
            ],
            cost_estimate=cost(2 * rows * width * entries, 2 * width * entries, rows * entries),
            compiler_params=params(24),
        )(*refs, *tables)

    up_2, down_2 = step_on(up_1, down_1)
    near = score([[up_1], [down_1]], near_tables, near_steps)
    up_2, down_2, near = lax.optimization_barrier((up_2, down_2, near))
    up_3, down_3 = step_on(up_2, down_2)
    up_2, down_2, *far = lax.optimization_barrier((up_2, down_2, *far))
    far_table = joined(far)
    far_tables = [far_table, shift(far_table, "c", 1)]
    middle = score([[up_2], [down_2]], near_tables, near_steps)
    up_3, down_3, middle = lax.optimization_barrier((up_3, down_3, middle))
    across = step_on(up_3[:, :half], down_3[:, half:])
    all_tables, all_steps = near_tables + far_tables, near_steps + far_steps
    outer = score([[up_3], [down_3]], all_tables, all_steps)
    distant = score([[up_1], [down_1], [up_2], [down_2]], far_tables, far_steps)
    across, outer, distant = lax.optimization_barrier((across, outer, distant))
    last = score([[chunk], across], all_tables, all_steps)

    members = size["z"] * size["x"]
    message, shares = pl.pallas_call(
        message_kernel,
        out_shape=(
            jax.ShapeDtypeStruct((members, 8, LANES), F32),
            jax.ShapeDtypeStruct((2, 8, LANES), F32),
        ),
        in_specs=[VMEM] * 5,
        out_specs=(VMEM, VMEM),
        cost_estimate=cost(1_000_000),
        compiler_params=params(4),
    )(near, middle, distant, outer, last)
    everyone = lax.all_to_all(message, ("z", "x"), 0, 0, tiled=True)
    groups = size["y"] * size["c"]
    group = pl.pallas_call(
        merge_kernel,
        out_shape=jax.ShapeDtypeStruct((groups, 8, LANES), F32),
        in_specs=[VMEM, VMEM],
        out_specs=VMEM,
        cost_estimate=cost(1_000_000),
        compiler_params=params(4),
    )(everyone, shares)
    group = lax.all_to_all(group, ("y", "c"), 0, 0, tiled=True)
    log_ppl, margin = pl.pallas_call(
        select_kernel,
        out_shape=(jax.ShapeDtypeStruct((2,), F32), jax.ShapeDtypeStruct((2,), F32)),
        in_specs=[SMEM, VMEM],
        out_specs=(SMEM, SMEM),
        cost_estimate=cost(1_000_000),
        compiler_params=params(4),
    )(cutoff, group)
    return (log_ppl, margin)


def solution(mesh):
    finer = Mesh(mesh.devices.reshape(8, 4, 2, mesh.shape["vocab"]), AXES)

    return jax.shard_map(
        on_device,
        mesh=finer,
        in_specs=(
            P(AXES, None, None),
            P(AXES, None),
            P(AXES),
            P(),
            P(),
            P(None, "x"),
            P(None, "x"),
            P("x", None),
            P(),
            P(AXES, None),
        ),
        out_specs=(P(AXES), P(AXES)),
        check_vma=False,
    )
```

profile of v0, /device:TPU:1, one launch (start us, length us, event | category | flops | bytes accessed | tf_op | source)
XLA Modules:
  0.0 107.3 jit_solution(13912912670659893897)
XLA Ops:
  0.6 2.2 %collective-permute-start.13 = (bf16[512,1024]{1,0:T(8,128)(2,1)}, bf16[512,1024]{1,0:T(8,128)(2,1)S(1)}, u32[]{:S(2)}, u32[]{:S(2)}) collective-permute-start(bf16[512,1024]{1,0:T(8,128)(2,1)} %refs_0_.2), channel_id=1, source_target_pairs={{0,8},{8,16},{16,24},{24,0},{1,9},{9,17},{17,25},{25,1},{2,10},{10... | collective-permute-start | bytes 3145736 | tf_op jit(solution)/shard_map/ppermute | solution.py:33
  2.8 1.5 %collective-permute-start.14 = (bf16[512,1024]{1,0:T(8,128)(2,1)}, bf16[512,1024]{1,0:T(8,128)(2,1)S(1)}, u32[]{:S(2)}, u32[]{:S(2)}) collective-permute-start(bf16[512,1024]{1,0:T(8,128)(2,1)} %refs_0_.2), channel_id=1, source_target_pairs={{0,24},{8,0},{16,8},{24,16},{1,25},{9,1},{17,9},{25,17},{2,26},{10... | collective-permute-start | bytes 3145736 | tf_op jit(solution)/shard_map/ppermute | solution.py:33
  4.4 1.2 %shard_map.113 = (bf16[40,1024]{1,0:T(8,128)(2,1)S(1)}, bf16[32,1024]{1,0:T(8,128)(2,1)S(1)}) custom-call(s32[2]{0:T(128)} %lengths_ref.1, s32[2,24]{1,0:T(2,128)} %tokens_ref.1, bf16[2,24,1024]{2,1,0:T(8,128)(2,1)} %hidden_ref.1, f32[1,1024]{1,0:T(1,128)} %bitcast.3), custom_call_target="tpu_custom_call" | custom-call | flops 4000000 | tf_op jit(solution)/shard_map/pallas_call | solution.py:295
  5.5 2.6 %collective-permute-start = (bf16[40,1024]{1,0:T(8,128)(2,1)S(1)}, bf16[40,1024]{1,0:T(8,128)(2,1)S(1)}, u32[]{:S(2)}, u32[]{:S(2)}) collective-permute-start(bf16[40,1024]{1,0:T(8,128)(2,1)S(1)} %get-tuple-element.34.refs_0_), channel_id=1, source_target_pairs={{0,3},{1,0},{2,1},{3,2},{4,7},{5,4},{6,5},{7,6},{8,11},{9,8},{10,9... | collective-permute-start | bytes 245768 | tf_op jit(solution)/shard_map/ppermute | solution.py:33
  8.1 0.5 collective-permute-start.1
  8.6 0.6 collective-permute-start.2
  9.2 2.9 %shard_map.114 = (bf16[1024,1024]{1,0:T(8,128)(2,1)S(1)}, bf16[1024,1024]{1,0:T(8,128)(2,1)S(1)}, bf16[1024,1024]{1,0:T(8,128)(2,1)S(1)}) custom-call(bf16[1024,1024]{1,0:T(8,128)(2,1)} %refs_0_.1, bf16[1024,1024]{1,0:T(8,128)(2,1)} %refs_1_, bf16[1024,1024]{1,0:T(8,128)(2,1)} %refs_2_), custom_call_target="tpu_custom_call" | custom-call | flops 3000000 | bytes 6300000 | tf_op jit(solution)/shard_map/pallas_call | solution.py:307
  12.1 0.0 collective-permute-done.refs_1_
  12.1 0.8 collective-permute-done.1.refs_2_
  12.9 1.1 %collective-permute-done.2.refs_3_ = bf16[40,1024]{1,0:T(8,128)(2,1)S(1)} collective-permute-done((bf16[40,1024]{1,0:T(8,128)(2,1)S(1)}, bf16[40,1024]{1,0:T(8,128)(2,1)S(1)}, u32[]{:S(2)}, u32[]{:S(2)}) %collective-permute-start.2) | collective-permute-done | bytes 81952 | tf_op jit(solution)/shard_map/ppermute | solution.py:33
  14.1 1.1 %shard_map.115 = (f32[32,1024]{1,0:T(8,128)S(1)}, bf16[32,1024]{1,0:T(8,128)(2,1)S(1)}, bf16[32,1024]{1,0:T(8,128)(2,1)S(1)}, bf16[32,1024]{1,0:T(8,128)(2,1)S(1)}, bf16[8,1024]{1,0:T(8,128)(2,1)S(1)}) custom-call(bf16[40,1024]{1,0:T(8,128)(2,1)S(1)} %get-tuple-element.34.refs_0_, bf16[40,1024]{1,0:T(8,128)(2,1)S(1)} %collective-permute-done.refs_1_, ...), custom_call_target="tpu_custom_call" | custom-call | flops 800000000 | bytes 6300000 | tf_op jit(solution)/shard_map/pallas_call | solution.py:318
  15.2 0.1 collective-permute-start.3
  15.3 1.5 %collective-permute-start.4 = (bf16[32,1024]{1,0:T(8,128)(2,1)S(1)}, bf16[32,1024]{1,0:T(8,128)(2,1)S(1)}, u32[]{:S(2)}, u32[]{:S(2)}) collective-permute-start(bf16[32,1024]{1,0:T(8,128)(2,1)S(1)} %get-tuple-element.43), channel_id=1, source_target_pairs={{0,2},{1,3},{2,0},{3,1},{4,6},{5,7},{6,4},{7,5},{8,10},{9,11},{10,... | collective-permute-start | bytes 196616 | tf_op jit(solution)/shard_map/ppermute | solution.py:33
  16.7 1.2 %collective-permute-start.5 = (bf16[32,1024]{1,0:T(8,128)(2,1)S(1)}, bf16[32,1024]{1,0:T(8,128)(2,1)S(1)}, u32[]{:S(2)}, u32[]{:S(2)}) collective-permute-start(bf16[32,1024]{1,0:T(8,128)(2,1)S(1)} %get-tuple-element.44), channel_id=1, source_target_pairs={{0,3},{1,0},{2,1},{3,2},{4,7},{5,4},{6,5},{7,6},{8,11},{9,8},{10,9... | collective-permute-start | bytes 196616 | tf_op jit(solution)/shard_map/ppermute | solution.py:33
  17.9 2.6 %collective-permute-done.3.first_ref = bf16[32,1024]{1,0:T(8,128)(2,1)S(1)} collective-permute-done((bf16[32,1024]{1,0:T(8,128)(2,1)S(1)}, bf16[32,1024]{1,0:T(8,128)(2,1)S(1)}, u32[]{:S(2)}, u32[]{:S(2)}) %collective-permute-start.3) | collective-permute-done | bytes 65568 | tf_op jit(solution)/shard_map/ppermute | solution.py:33
  20.6 0.0 collective-permute-done.4.second_ref
  20.6 0.6 collective-permute-done.5.third_ref
  21.2 0.0 copy-done.1
  21.2 0.1 shard_map.116.refs_0_
  21.3 2.2 %collective-permute-start.6 = (bf16[32,1024]{1,0:T(8,128)(2,1)S(1)}, bf16[32,1024]{1,0:T(8,128)(2,1)S(1)}, u32[]{:S(2)}, u32[]{:S(2)}) collective-permute-start(bf16[32,1024]{1,0:T(8,128)(2,1)S(1)} %shard_map.116.refs_0_), channel_id=1, source_target_pairs={{0,3},{1,0},{2,1},{3,2},{4,7},{5,4},{6,5},{7,6},{8,11},{9,8},{10,9... | collective-permute-start | bytes 196616 | tf_op jit(solution)/shard_map/ppermute | solution.py:33
  23.5 0.4 collective-permute-start.7
  23.9 0.2 collective-permute-start.8
  24.2 0.7 collective-permute-done.6.refs_1_
  24.8 3.3 %collective-permute-done.7.refs_2_ = bf16[32,1024]{1,0:T(8,128)(2,1)S(1)} collective-permute-done((bf16[32,1024]{1,0:T(8,128)(2,1)S(1)}, bf16[32,1024]{1,0:T(8,128)(2,1)S(1)}, u32[]{:S(2)}, u32[]{:S(2)}) %collective-permute-start.7) | collective-permute-done | bytes 65568 | tf_op jit(solution)/shard_map/ppermute | solution.py:33
  28.2 0.6 collective-permute-done.8.refs_3_
  28.8 0.0 collective-permute-done.13.refs_1_
  28.8 0.0 collective-permute-done.14.refs_2_
  28.9 0.2 shard_map.118.refs_2_.refs_3_
  29.1 5.2 %collective-permute-start.15 = (bf16[1536,1024]{1,0:T(8,128)(2,1)S(1)}, bf16[1536,1024]{1,0:T(8,128)(2,1)S(1)}, u32[]{:S(2)}, u32[]{:S(2)}) collective-permute-start(bf16[1536,1024]{1,0:T(8,128)(2,1)S(1)} %shard_map.118.refs_2_.refs_3_), channel_id=1, source_target_pairs={{0,4},{4,0},{1,5},{5,1},{2,6},{6,2},{3,7},{7,3},{8,12},{12,8},{9,1... | collective-permute-start | bytes 9437192 | tf_op jit(solution)/shard_map/ppermute | solution.py:33
  34.3 1.6 %collective-permute-start.9 = (bf16[136,1024]{1,0:T(8,128)(2,1)S(1)}, bf16[136,1024]{1,0:T(8,128)(2,1)S(1)}, u32[]{:S(2)}, u32[]{:S(2)}) collective-permute-start(bf16[136,1024]{1,0:T(8,128)(2,1)S(1)} %shard_map.117.refs_0_), channel_id=1, source_target_pairs={{0,32},{32,64},{64,96},{96,128},{128,160},{160,192},{192,224},{224... | collective-permute-start | bytes 835592 | tf_op jit(solution)/shard_map/ppermute | solution.py:33
  35.9 4.0 %collective-permute-start.11 = (bf16[136,1024]{1,0:T(8,128)(2,1)S(1)}, bf16[136,1024]{1,0:T(8,128)(2,1)S(1)}, u32[]{:S(2)}, u32[]{:S(2)}) collective-permute-start(bf16[136,1024]{1,0:T(8,128)(2,1)S(1)} %shard_map.117.refs_0_), channel_id=1, source_target_pairs={{0,224},{32,0},{64,32},{96,64},{128,96},{160,128},{192,160},{224,1... | collective-permute-start | bytes 835592 | tf_op jit(solution)/shard_map/ppermute | solution.py:33
  39.9 0.5 collective-permute-start.18
  40.4 2.2 %collective-permute-start.19 = (bf16[256,1024]{1,0:T(8,128)(2,1)S(1)}, bf16[256,1024]{1,0:T(8,128)(2,1)S(1)}, u32[]{:S(2)}, u32[]{:S(2)}) collective-permute-start(bf16[256,1024]{1,0:T(8,128)(2,1)S(1)} %slice.13), channel_id=1, source_target_pairs={{0,24},{8,0},{16,8},{24,16},{1,25},{9,1},{17,9},{25,17},{2,26},{10... | collective-permute-start | bytes 1572872 | tf_op jit(solution)/shard_map/ppermute | solution.py:33
  42.7 4.1 %collective-permute-done.9.refs_0_ = bf16[136,1024]{1,0:T(8,128)(2,1)S(1)} collective-permute-done((bf16[136,1024]{1,0:T(8,128)(2,1)S(1)}, bf16[136,1024]{1,0:T(8,128)(2,1)S(1)}, u32[]{:S(2)}, u32[]{:S(2)}) %collective-permute-start.9) | collective-permute-done | bytes 278560 | tf_op jit(solution)/shard_map/ppermute | solution.py:33
  46.8 0.0 collective-permute-start.10
  46.8 0.0 collective-permute-done.11.refs_1_
  46.8 2.7 %collective-permute-start.12 = (bf16[136,1024]{1,0:T(8,128)(2,1)S(1)}, bf16[136,1024]{1,0:T(8,128)(2,1)S(1)}, u32[]{:S(2)}, u32[]{:S(2)}) collective-permute-start(bf16[136,1024]{1,0:T(8,128)(2,1)S(1)} %collective-permute-done.11.refs_1_), channel_id=1, source_target_pairs={{0,224},{32,0},{64,32},{96,64},{128,96},{160,128},{192,160},{224,1... | collective-permute-start | bytes 835592 | tf_op jit(solution)/shard_map/ppermute | solution.py:33
  49.5 0.0 collective-permute-done.15.refs_3_.refs_4_
  49.5 2.4 %shard_map.119.near_ref = f32[2,8,128]{2,1,0:T(8,128)S(1)} custom-call(bf16[136,1024]{1,0:T(8,128)(2,1)S(1)} %collective-permute-done.9.refs_0_, bf16[136,1024]{1,0:T(8,128)(2,1)S(1)} %collective-permute-done.11.refs_1_, bf16[1536,1024]{1,0:T(8,128)(2,1)S(1)} %shard_map.118.refs_2_.refs_3_, bf16[1536,1024]{1,0:T(8,128)(2,1)S(1)} %collective-permute-done.15.refs_3_.refs_4_), custom_call_target="tpu_custom_call" | custom-call | flops 1610612736 | bytes 6291456 | tf_op jit(solution)/shard_map/pallas_call | solution.py:376
  51.9 3.7 %collective-permute-done.10.refs_0_.refs_2_ = bf16[136,1024]{1,0:T(8,128)(2,1)S(1)} collective-permute-done((bf16[136,1024]{1,0:T(8,128)(2,1)S(1)}, bf16[136,1024]{1,0:T(8,128)(2,1)S(1)}, u32[]{:S(2)}, u32[]{:S(2)}) %collective-permute-start.10) | collective-permute-done | bytes 278560 | tf_op jit(solution)/shard_map/ppermute | solution.py:33
  55.5 0.0 collective-permute-done.12.refs_1_.refs_3_
  55.5 0.0 collective-permute-done.18.refs_0_
  55.6 0.0 collective-permute-done.19.refs_1_
  55.6 0.1 shard_map.121.refs_4_.refs_5_
  55.6 1.6 %collective-permute-start.22 = (bf16[512,1024]{1,0:T(8,128)(2,1)S(1)}, bf16[512,1024]{1,0:T(8,128)(2,1)S(1)}, u32[]{:S(2)}, u32[]{:S(2)}) collective-permute-start(bf16[512,1024]{1,0:T(8,128)(2,1)S(1)} %shard_map.121.refs_4_.refs_5_), channel_id=1, source_target_pairs={{0,4},{4,0},{1,5},{5,1},{2,6},{6,2},{3,7},{7,3},{8,12},{12,8},{9,1... | collective-permute-start | bytes 3145736 | tf_op jit(solution)/shard_map/ppermute | solution.py:33
  57.2 0.0 collective-permute-start.16
  57.3 2.7 %collective-permute-start.17 = (bf16[136,1024]{1,0:T(8,128)(2,1)S(1)}, bf16[136,1024]{1,0:T(8,128)(2,1)S(1)}, u32[]{:S(2)}, u32[]{:S(2)}) collective-permute-start(bf16[136,1024]{1,0:T(8,128)(2,1)S(1)} %collective-permute-done.12.refs_1_.refs_3_), channel_id=1, source_target_pairs={{0,224},{32,0},{64,32},{96,64},{128,96},{160,128},{192,160},{224,1... | collective-permute-start | bytes 835592 | tf_op jit(solution)/shard_map/ppermute | solution.py:33
  59.9 2.4 %shard_map.120.middle_ref = f32[2,8,128]{2,1,0:T(8,128)S(1)} custom-call(bf16[136,1024]{1,0:T(8,128)(2,1)S(1)} %collective-permute-done.10.refs_0_.refs_2_, bf16[136,1024]{1,0:T(8,128)(2,1)S(1)} %collective-permute-done.12.refs_1_.refs_3_, bf16[1536,1024]{1,0:T(8,128)(2,1)S(1)} %shard_map.118.refs_2_.refs_3_, ...), custom_call_target="tpu_custom_call" | custom-call | flops 1610612736 | bytes 6291456 | tf_op jit(solution)/shard_map/pallas_call | solution.py:376
  62.3 4.3 %collective-permute-done.16.refs_0_ = bf16[136,1024]{1,0:T(8,128)(2,1)S(1)} collective-permute-done((bf16[136,1024]{1,0:T(8,128)(2,1)S(1)}, bf16[136,1024]{1,0:T(8,128)(2,1)S(1)}, u32[]{:S(2)}, u32[]{:S(2)}) %collective-permute-start.16) | collective-permute-done | bytes 278560 | tf_op jit(solution)/shard_map/ppermute | solution.py:33
  66.6 0.0 collective-permute-done.17.refs_1_
  66.6 2.0 %collective-permute-start.20 = (bf16[136,512]{1,0:T(8,128)(2,1)S(1)}, bf16[136,512]{1,0:T(8,128)(2,1)S(1)}, u32[]{:S(2)}, u32[]{:S(2)}) collective-permute-start(bf16[136,512]{1,0:T(8,128)(2,1)S(1)} %slice.14), channel_id=1, source_target_pairs={{0,32},{32,64},{64,96},{96,128},{128,160},{160,192},{192,224},{224... | collective-permute-start | bytes 417800 | tf_op jit(solution)/shard_map/ppermute | solution.py:33
  68.6 1.1 %collective-permute-start.21 = (bf16[136,512]{1,0:T(8,128)(2,1)S(1)}, bf16[136,512]{1,0:T(8,128)(2,1)S(1)}, u32[]{:S(2)}, u32[]{:S(2)}) collective-permute-start(bf16[136,512]{1,0:T(8,128)(2,1)S(1)} %slice.15), channel_id=1, source_target_pairs={{0,224},{32,0},{64,32},{96,64},{128,96},{160,128},{192,160},{224,1... | collective-permute-start | bytes 417800 | tf_op jit(solution)/shard_map/ppermute | solution.py:33
  69.7 0.0 collective-permute-done.22.refs_5_.refs_6_
  69.7 3.1 %shard_map.122.outer_ref = f32[2,8,128]{2,1,0:T(8,128)S(1)} custom-call(bf16[136,1024]{1,0:T(8,128)(2,1)S(1)} %collective-permute-done.16.refs_0_, bf16[136,1024]{1,0:T(8,128)(2,1)S(1)} %collective-permute-done.17.refs_1_, bf16[1536,1024]{1,0:T(8,128)(2,1)S(1)} %shard_map.118.refs_2_.refs_3_, bf16[1536,1024]{1,0:T(8,128)(2,1)S(1)} %collective-permute-done.15.refs_3_.refs_4_, ...), custom_call_target="tpu_custom_call" | custom-call | flops 2147483648 | bytes 8388608 | tf_op jit(solution)/shard_map/pallas_call | solution.py:376
  72.8 2.0 %shard_map.123.far_ref = f32[4,8,128]{2,1,0:T(8,128)S(1)} custom-call(bf16[136,1024]{1,0:T(8,128)(2,1)S(1)} %collective-permute-done.9.refs_0_, bf16[136,1024]{1,0:T(8,128)(2,1)S(1)} %collective-permute-done.11.refs_1_, bf16[136,1024]{1,0:T(8,128)(2,1)S(1)} %collective-permute-done.10.refs_0_.refs_2_, ...), custom_call_target="tpu_custom_call" | custom-call | flops 1073741824 | bytes 2097152 | tf_op jit(solution)/shard_map/pallas_call | solution.py:376
  74.9 0.0 collective-permute-done.20.refs_1_
  74.9 0.0 collective-permute-done.21.refs_2_
  74.9 3.1 %shard_map.124.last_ref = f32[2,8,128]{2,1,0:T(8,128)S(1)} custom-call(bf16[136,1024]{1,0:T(8,128)(2,1)S(1)} %shard_map.117.refs_0_, bf16[136,512]{1,0:T(8,128)(2,1)S(1)} %collective-permute-done.20.refs_1_, bf16[136,512]{1,0:T(8,128)(2,1)S(1)} %collective-permute-done.21.refs_2_, bf16[1536,1024]{1,0:T(8,128)(2,1)S(1)} %shard_map.118.refs_2_.refs_3_, ...), custom_call_target="tpu_custom_call" | custom-call | flops 2147483648 | bytes 8388608 | tf_op jit(solution)/shard_map/pallas_call | solution.py:376
  78.0 0.3 shard_map.125
  78.3 15.3 %all_to_all.10.everyone_ref = f32[32,8,128]{2,1,0:T(8,128)S(1)} all-to-all(f32[32,8,128]{2,1,0:T(8,128)S(1)} %get-tuple-element.64), channel_id=1, replica_groups=mesh['z'=8,'y'=4,'c'=2,'x'=4] {'z','x'}, dimensions={0} | all-to-all | bytes 262144 | tf_op jit(solution)/shard_map/all_to_all | solution.py:418
  93.6 0.9 shard_map.126
  94.5 6.4 %all-to-all-start.1 = ((f32[8,8,128]{2,1,0:T(8,128)}), f32[8,8,128]{2,1,0:T(8,128)S(1)}, u32[]{:S(2)}, u32[]{:S(2)}) async-start(f32[8,8,128]{2,1,0:T(8,128)} %shard_map.126), calls=%async_computation.1 | async-start | bytes 65536 | tf_op jit(solution)/shard_map/all_to_all | solution.py:428
  101.5 4.1 %all-to-all-done.1.groups_ref = f32[8,8,128]{2,1,0:T(8,128)S(1)} async-done(((f32[8,8,128]{2,1,0:T(8,128)}), f32[8,8,128]{2,1,0:T(8,128)S(1)}, u32[]{:S(2)}, u32[]{:S(2)}) %all-to-all-start.1) | async-done | bytes 32800 | tf_op jit(solution)/shard_map/all_to_all | solution.py:428
  105.6 1.5 %shard_map.127 = (f32[2]{0:T(128)}, f32[2]{0:T(128)}) custom-call(s32[1]{0:T(128)S(6)} %copy.12.cutoff_ref, f32[8,8,128]{2,1,0:T(8,128)S(1)} %all-to-all-done.1.groups_ref), custom_call_target="tpu_custom_call" | custom-call | flops 1000000 | tf_op jit(solution)/shard_map/pallas_call | solution.py:429
  (8 shorter events, 0.1 us)
Async XLA Ops:
  0.6 28.2 %collective-permute-start.13 = (bf16[512,1024]{1,0:T(8,128)(2,1)}, bf16[512,1024]{1,0:T(8,128)(2,1)S(1)}, u32[]{:S(2)}, u32[]{:S(2)}) collective-permute-start(bf16[512,1024]{1,0:T(8,128)(2,1)} %refs_0_.2), channel_id=1, source_target_pairs={{0,8},{8,16},{16,24},{24,0},{1,9},{9,17},{17,25},{25,1},{2,10},{10... | collective-permute-start | bytes 3145736 | tf_op jit(solution)/shard_map/ppermute | solution.py:33
  2.8 26.0 %collective-permute-start.14 = (bf16[512,1024]{1,0:T(8,128)(2,1)}, bf16[512,1024]{1,0:T(8,128)(2,1)S(1)}, u32[]{:S(2)}, u32[]{:S(2)}) collective-permute-start(bf16[512,1024]{1,0:T(8,128)(2,1)} %refs_0_.2), channel_id=1, source_target_pairs={{0,24},{8,0},{16,8},{24,16},{1,25},{9,1},{17,9},{25,17},{2,26},{10... | collective-permute-start | bytes 3145736 | tf_op jit(solution)/shard_map/ppermute | solution.py:33
  5.5 6.6 %collective-permute-start = (bf16[40,1024]{1,0:T(8,128)(2,1)S(1)}, bf16[40,1024]{1,0:T(8,128)(2,1)S(1)}, u32[]{:S(2)}, u32[]{:S(2)}) collective-permute-start(bf16[40,1024]{1,0:T(8,128)(2,1)S(1)} %get-tuple-element.34.refs_0_), channel_id=1, source_target_pairs={{0,3},{1,0},{2,1},{3,2},{4,7},{5,4},{6,5},{7,6},{8,11},{9,8},{10,9... | collective-permute-start | bytes 245768 | tf_op jit(solution)/shard_map/ppermute | solution.py:33
  8.1 4.9 %collective-permute-start.1 = (bf16[40,1024]{1,0:T(8,128)(2,1)S(1)}, bf16[40,1024]{1,0:T(8,128)(2,1)S(1)}, u32[]{:S(2)}, u32[]{:S(2)}) collective-permute-start(bf16[40,1024]{1,0:T(8,128)(2,1)S(1)} %get-tuple-element.34.refs_0_), channel_id=1, source_target_pairs={{0,2},{1,3},{2,0},{3,1},{4,6},{5,7},{6,4},{7,5},{8,10},{9,11},{10,... | collective-permute-start | bytes 245768 | tf_op jit(solution)/shard_map/ppermute | solution.py:33
  8.6 5.4 %collective-permute-start.2 = (bf16[40,1024]{1,0:T(8,128)(2,1)S(1)}, bf16[40,1024]{1,0:T(8,128)(2,1)S(1)}, u32[]{:S(2)}, u32[]{:S(2)}) collective-permute-start(bf16[40,1024]{1,0:T(8,128)(2,1)S(1)} %get-tuple-element.34.refs_0_), channel_id=1, source_target_pairs={{0,1},{1,2},{2,3},{3,0},{4,5},{5,6},{6,7},{7,4},{8,9},{9,10},{10,1... | collective-permute-start | bytes 245768 | tf_op jit(solution)/shard_map/ppermute | solution.py:33
  14.1 7.1 %copy-start.1 = (f32[1024]{0:T(1024)S(1)}, f32[1024]{0:T(1024)}, u32[]{:S(2)}) copy-start(f32[1024]{0:T(1024)} %param.18) | copy-start | bytes 12292
  14.1 14.8 %copy-start = (bf16[512,1024]{1,0:T(8,128)(2,1)S(1)}, bf16[512,1024]{1,0:T(8,128)(2,1)}, u32[]{:S(2)}) copy-start(bf16[512,1024]{1,0:T(8,128)(2,1)} %refs_0_.2) | copy-start | bytes 3145732
  15.2 5.4 %collective-permute-start.3 = (bf16[32,1024]{1,0:T(8,128)(2,1)S(1)}, bf16[32,1024]{1,0:T(8,128)(2,1)S(1)}, u32[]{:S(2)}, u32[]{:S(2)}) collective-permute-start(bf16[32,1024]{1,0:T(8,128)(2,1)S(1)} %get-tuple-element.42), channel_id=1, source_target_pairs={{0,1},{1,2},{2,3},{3,0},{4,5},{5,6},{6,7},{7,4},{8,9},{9,10},{10,1... | collective-permute-start | bytes 196616 | tf_op jit(solution)/shard_map/ppermute | solution.py:33
  15.3 5.3 %collective-permute-start.4 = (bf16[32,1024]{1,0:T(8,128)(2,1)S(1)}, bf16[32,1024]{1,0:T(8,128)(2,1)S(1)}, u32[]{:S(2)}, u32[]{:S(2)}) collective-permute-start(bf16[32,1024]{1,0:T(8,128)(2,1)S(1)} %get-tuple-element.43), channel_id=1, source_target_pairs={{0,2},{1,3},{2,0},{3,1},{4,6},{5,7},{6,4},{7,5},{8,10},{9,11},{10,... | collective-permute-start | bytes 196616 | tf_op jit(solution)/shard_map/ppermute | solution.py:33
  16.7 4.4 %collective-permute-start.5 = (bf16[32,1024]{1,0:T(8,128)(2,1)S(1)}, bf16[32,1024]{1,0:T(8,128)(2,1)S(1)}, u32[]{:S(2)}, u32[]{:S(2)}) collective-permute-start(bf16[32,1024]{1,0:T(8,128)(2,1)S(1)} %get-tuple-element.44), channel_id=1, source_target_pairs={{0,3},{1,0},{2,1},{3,2},{4,7},{5,4},{6,5},{7,6},{8,11},{9,8},{10,9... | collective-permute-start | bytes 196616 | tf_op jit(solution)/shard_map/ppermute | solution.py:33
  21.3 3.5 %collective-permute-start.6 = (bf16[32,1024]{1,0:T(8,128)(2,1)S(1)}, bf16[32,1024]{1,0:T(8,128)(2,1)S(1)}, u32[]{:S(2)}, u32[]{:S(2)}) collective-permute-start(bf16[32,1024]{1,0:T(8,128)(2,1)S(1)} %shard_map.116.refs_0_), channel_id=1, source_target_pairs={{0,3},{1,0},{2,1},{3,2},{4,7},{5,4},{6,5},{7,6},{8,11},{9,8},{10,9... | collective-permute-start | bytes 196616 | tf_op jit(solution)/shard_map/ppermute | solution.py:33
  23.5 4.7 %collective-permute-start.7 = (bf16[32,1024]{1,0:T(8,128)(2,1)S(1)}, bf16[32,1024]{1,0:T(8,128)(2,1)S(1)}, u32[]{:S(2)}, u32[]{:S(2)}) collective-permute-start(bf16[32,1024]{1,0:T(8,128)(2,1)S(1)} %shard_map.116.refs_0_), channel_id=1, source_target_pairs={{0,2},{1,3},{2,0},{3,1},{4,6},{5,7},{6,4},{7,5},{8,10},{9,11},{10,... | collective-permute-start | bytes 196616 | tf_op jit(solution)/shard_map/ppermute | solution.py:33
  23.9 4.9 %collective-permute-start.8 = (bf16[32,1024]{1,0:T(8,128)(2,1)S(1)}, bf16[32,1024]{1,0:T(8,128)(2,1)S(1)}, u32[]{:S(2)}, u32[]{:S(2)}) collective-permute-start(bf16[32,1024]{1,0:T(8,128)(2,1)S(1)} %shard_map.116.refs_0_), channel_id=1, source_target_pairs={{0,1},{1,2},{2,3},{3,0},{4,5},{5,6},{6,7},{7,4},{8,9},{9,10},{10,1... | collective-permute-start | bytes 196616 | tf_op jit(solution)/shard_map/ppermute | solution.py:33
  29.1 20.4 %collective-permute-start.15 = (bf16[1536,1024]{1,0:T(8,128)(2,1)S(1)}, bf16[1536,1024]{1,0:T(8,128)(2,1)S(1)}, u32[]{:S(2)}, u32[]{:S(2)}) collective-permute-start(bf16[1536,1024]{1,0:T(8,128)(2,1)S(1)} %shard_map.118.refs_2_.refs_3_), channel_id=1, source_target_pairs={{0,4},{4,0},{1,5},{5,1},{2,6},{6,2},{3,7},{7,3},{8,12},{12,8},{9,1... | collective-permute-start | bytes 9437192 | tf_op jit(solution)/shard_map/ppermute | solution.py:33
  34.3 12.5 %collective-permute-start.9 = (bf16[136,1024]{1,0:T(8,128)(2,1)S(1)}, bf16[136,1024]{1,0:T(8,128)(2,1)S(1)}, u32[]{:S(2)}, u32[]{:S(2)}) collective-permute-start(bf16[136,1024]{1,0:T(8,128)(2,1)S(1)} %shard_map.117.refs_0_), channel_id=1, source_target_pairs={{0,32},{32,64},{64,96},{96,128},{128,160},{160,192},{192,224},{224... | collective-permute-start | bytes 835592 | tf_op jit(solution)/shard_map/ppermute | solution.py:33
  35.9 10.9 %collective-permute-start.11 = (bf16[136,1024]{1,0:T(8,128)(2,1)S(1)}, bf16[136,1024]{1,0:T(8,128)(2,1)S(1)}, u32[]{:S(2)}, u32[]{:S(2)}) collective-permute-start(bf16[136,1024]{1,0:T(8,128)(2,1)S(1)} %shard_map.117.refs_0_), channel_id=1, source_target_pairs={{0,224},{32,0},{64,32},{96,64},{128,96},{160,128},{192,160},{224,1... | collective-permute-start | bytes 835592 | tf_op jit(solution)/shard_map/ppermute | solution.py:33
  39.9 15.6 %collective-permute-start.18 = (bf16[256,1024]{1,0:T(8,128)(2,1)S(1)}, bf16[256,1024]{1,0:T(8,128)(2,1)S(1)}, u32[]{:S(2)}, u32[]{:S(2)}) collective-permute-start(bf16[256,1024]{1,0:T(8,128)(2,1)S(1)} %slice.12), channel_id=1, source_target_pairs={{0,8},{8,16},{16,24},{24,0},{1,9},{9,17},{17,25},{25,1},{2,10},{10... | collective-permute-start | bytes 1572872 | tf_op jit(solution)/shard_map/ppermute | solution.py:33
  40.4 15.1 %collective-permute-start.19 = (bf16[256,1024]{1,0:T(8,128)(2,1)S(1)}, bf16[256,1024]{1,0:T(8,128)(2,1)S(1)}, u32[]{:S(2)}, u32[]{:S(2)}) collective-permute-start(bf16[256,1024]{1,0:T(8,128)(2,1)S(1)} %slice.13), channel_id=1, source_target_pairs={{0,24},{8,0},{16,8},{24,16},{1,25},{9,1},{17,9},{25,17},{2,26},{10... | collective-permute-start | bytes 1572872 | tf_op jit(solution)/shard_map/ppermute | solution.py:33
  46.8 8.8 %collective-permute-start.10 = (bf16[136,1024]{1,0:T(8,128)(2,1)S(1)}, bf16[136,1024]{1,0:T(8,128)(2,1)S(1)}, u32[]{:S(2)}, u32[]{:S(2)}) collective-permute-start(bf16[136,1024]{1,0:T(8,128)(2,1)S(1)} %collective-permute-done.9.refs_0_), channel_id=1, source_target_pairs={{0,32},{32,64},{64,96},{96,128},{128,160},{160,192},{192,224},{224... | collective-permute-start | bytes 835592 | tf_op jit(solution)/shard_map/ppermute | solution.py:33
  46.8 8.8 %collective-permute-start.12 = (bf16[136,1024]{1,0:T(8,128)(2,1)S(1)}, bf16[136,1024]{1,0:T(8,128)(2,1)S(1)}, u32[]{:S(2)}, u32[]{:S(2)}) collective-permute-start(bf16[136,1024]{1,0:T(8,128)(2,1)S(1)} %collective-permute-done.11.refs_1_), channel_id=1, source_target_pairs={{0,224},{32,0},{64,32},{96,64},{128,96},{160,128},{192,160},{224,1... | collective-permute-start | bytes 835592 | tf_op jit(solution)/shard_map/ppermute | solution.py:33
  55.6 14.0 %collective-permute-start.22 = (bf16[512,1024]{1,0:T(8,128)(2,1)S(1)}, bf16[512,1024]{1,0:T(8,128)(2,1)S(1)}, u32[]{:S(2)}, u32[]{:S(2)}) collective-permute-start(bf16[512,1024]{1,0:T(8,128)(2,1)S(1)} %shard_map.121.refs_4_.refs_5_), channel_id=1, source_target_pairs={{0,4},{4,0},{1,5},{5,1},{2,6},{6,2},{3,7},{7,3},{8,12},{12,8},{9,1... | collective-permute-start | bytes 3145736 | tf_op jit(solution)/shard_map/ppermute | solution.py:33
  57.2 9.3 %collective-permute-start.16 = (bf16[136,1024]{1,0:T(8,128)(2,1)S(1)}, bf16[136,1024]{1,0:T(8,128)(2,1)S(1)}, u32[]{:S(2)}, u32[]{:S(2)}) collective-permute-start(bf16[136,1024]{1,0:T(8,128)(2,1)S(1)} %collective-permute-done.10.refs_0_.refs_2_), channel_id=1, source_target_pairs={{0,32},{32,64},{64,96},{96,128},{128,160},{160,192},{192,224},{224... | collective-permute-start | bytes 835592 | tf_op jit(solution)/shard_map/ppermute | solution.py:33
  57.3 9.3 %collective-permute-start.17 = (bf16[136,1024]{1,0:T(8,128)(2,1)S(1)}, bf16[136,1024]{1,0:T(8,128)(2,1)S(1)}, u32[]{:S(2)}, u32[]{:S(2)}) collective-permute-start(bf16[136,1024]{1,0:T(8,128)(2,1)S(1)} %collective-permute-done.12.refs_1_.refs_3_), channel_id=1, source_target_pairs={{0,224},{32,0},{64,32},{96,64},{128,96},{160,128},{192,160},{224,1... | collective-permute-start | bytes 835592 | tf_op jit(solution)/shard_map/ppermute | solution.py:33
  66.6 8.3 %collective-permute-start.20 = (bf16[136,512]{1,0:T(8,128)(2,1)S(1)}, bf16[136,512]{1,0:T(8,128)(2,1)S(1)}, u32[]{:S(2)}, u32[]{:S(2)}) collective-permute-start(bf16[136,512]{1,0:T(8,128)(2,1)S(1)} %slice.14), channel_id=1, source_target_pairs={{0,32},{32,64},{64,96},{96,128},{128,160},{160,192},{192,224},{224... | collective-permute-start | bytes 417800 | tf_op jit(solution)/shard_map/ppermute | solution.py:33
  68.6 6.3 %collective-permute-start.21 = (bf16[136,512]{1,0:T(8,128)(2,1)S(1)}, bf16[136,512]{1,0:T(8,128)(2,1)S(1)}, u32[]{:S(2)}, u32[]{:S(2)}) collective-permute-start(bf16[136,512]{1,0:T(8,128)(2,1)S(1)} %slice.15), channel_id=1, source_target_pairs={{0,224},{32,0},{64,32},{96,64},{128,96},{160,128},{192,160},{224,1... | collective-permute-start | bytes 417800 | tf_op jit(solution)/shard_map/ppermute | solution.py:33
  94.5 11.1 %all-to-all-start.1 = ((f32[8,8,128]{2,1,0:T(8,128)}), f32[8,8,128]{2,1,0:T(8,128)S(1)}, u32[]{:S(2)}, u32[]{:S(2)}) async-start(f32[8,8,128]{2,1,0:T(8,128)} %shard_map.126), calls=%async_computation.1 | async-start | bytes 65536 | tf_op jit(solution)/shard_map/all_to_all | solution.py:428
where the time goes:
time: 108 us; the launch traced here: 107 us
  starting transfers between devices  42.9 us (40%)
  waiting for transfers between devices  25.9 us (24%)
  Pallas kernels  21.4 us (20%)
  blocking collectives  15.3 us (14%)
  between operations  1.64 us (2%)
    ppermute x23, starting transfers between devices, shift(): return lax.ppermute(array, axis, pairs)  36.5 us
    ppermute x23, waiting for transfers between devices, shift(): return lax.ppermute(array, axis, pairs)  21.9 us
    all_to_all x1, blocking collectives, on_device(): everyone = lax.all_to_all(message, ('z', 'x'), 0, 0, tiled=True)  15.3 us
    pallas_call x5, Pallas kernels, score(): pl.pallas_call(kernel, out_shape=jax.ShapeDtypeStruct((len(chunks), 8, LA...  13.1 us
    all_to_all x1, starting transfers between devices, on_device(): group = lax.all_to_all(group, ('y', 'c'), 0, 0, tiled=True)  6.37 us
    all_to_all x1, waiting for transfers between devices, on_device(): group = lax.all_to_all(group, ('y', 'c'), 0, 0, tiled=True)  4.07 us
    pallas_call x1, Pallas kernels, on_device(): pl.pallas_call(stage_kernel, out_shape=tuple((pltpu.VMEM(weight.shape, BF...  2.88 us
  transfers between devices with their start and end apart: 24, of which 11 were waited for; matrix products, arithmetic and copies ran while one was open for 0% of the time, Pallas kernels for 14%

commit v1 on v0

--- a/solution.py
+++ b/solution.py
@@ -243,13 +243,12 @@
     carried = iota((8, LANES), 1) % CAP >= CAP - 2
     lse = jnp.where(carried, 0.0, lse)
     sums = document_sums(weight_ref[0] * lse, weight_ref[1] * lse)
-    group = jnp.where(carried, sums - total, 0.0)
-    for k in range(out_ref.shape[0]):
-        out_ref[k] = group
-
-
-def select_kernel(cutoff_ref, groups_ref, log_ref, margin_ref):
-    values = groups_ref[...].reshape(-1, LANES)
+    out_ref[...] = jnp.where(carried, sums - total, 0.0)
+
+
+def select_kernel(cutoff_ref, *refs):
+    groups, (log_ref, margin_ref) = refs[:-2], refs[-2:]
+    values = jnp.concatenate([ref[...] for ref in groups], axis=0)
     across = values.T
     count = values.shape[0]
     lanes = [x * CAP + CAP - 2 + d for x in range(4) for d in range(2)]
@@ -264,7 +263,7 @@
             best, jnp.where(rank >= cutoff_ref[0].astype(F32), value, jnp.inf)
         )
     threshold = jnp.min(best)
-    own = groups_ref[lax.axis_index("y") * 2 + lax.axis_index("c")]
+    own = values[:8]
     row, lane_at = iota((8, LANES), 0), iota((8, LANES), 1)
     for d in range(2):
         here = (row == lax.axis_index("z")) & (
@@ -395,12 +394,12 @@
     far_table = joined(far)
     far_tables = [far_table, shift(far_table, "c", 1)]
     middle = score([[up_2], [down_2]], near_tables, near_steps)
-    up_3, down_3, middle = lax.optimization_barrier((up_3, down_3, middle))
+    distant = score([[up_1], [down_1], [up_2], [down_2]], far_tables, far_steps)
+    up_3, down_3, middle, distant = lax.optimization_barrier((up_3, down_3, middle, distant))
     across = step_on(up_3[:, :half], down_3[:, half:])
     all_tables, all_steps = near_tables + far_tables, near_steps + far_steps
     outer = score([[up_3], [down_3]], all_tables, all_steps)
-    distant = score([[up_1], [down_1], [up_2], [down_2]], far_tables, far_steps)
-    across, outer, distant = lax.optimization_barrier((across, outer, distant))
+    across, outer = lax.optimization_barrier((across, outer))
     last = score([[chunk], across], all_tables, all_steps)
 
     members = size["z"] * size["x"]
@@ -416,24 +415,23 @@
         compiler_params=params(4),
     )(near, middle, distant, outer, last)
     everyone = lax.all_to_all(message, ("z", "x"), 0, 0, tiled=True)
-    groups = size["y"] * size["c"]
     group = pl.pallas_call(
         merge_kernel,
-        out_shape=jax.ShapeDtypeStruct((groups, 8, LANES), F32),
+        out_shape=jax.ShapeDtypeStruct((8, LANES), F32),
         in_specs=[VMEM, VMEM],
         out_specs=VMEM,
         cost_estimate=cost(1_000_000),
         compiler_params=params(4),
     )(everyone, shares)
-    group = lax.all_to_all(group, ("y", "c"), 0, 0, tiled=True)
+    pair = jnp.concatenate([group, shift(group, "c", 1)], axis=0)
     log_ppl, margin = pl.pallas_call(
         select_kernel,
         out_shape=(jax.ShapeDtypeStruct((2,), F32), jax.ShapeDtypeStruct((2,), F32)),
-        in_specs=[SMEM, VMEM],
+        in_specs=[SMEM] + [VMEM] * 4,
         out_specs=(SMEM, SMEM),
         cost_estimate=cost(1_000_000),
         compiler_params=params(4),
-    )(cutoff, group)
+    )(cutoff, pair, *[shift(pair, "y", step) for step in (1, -1, 2)])
     return (log_ppl, margin)
 
 

time: 108 us -> 105 us (0.972)
  waiting for transfers between devices: 25.9 us -> 23.7 us
    ppermute x23 -> x27, starting transfers between devices: 36.5 us -> 43.2 us  [shift(): return lax.ppermute(array, axis, pairs)]
    all_to_all x1 -> x0, starting transfers between devices: 6.37 us -> none  [on_device(): group = lax.all_to_all(group, ('y', 'c'), 0, 0, tiled=True)]
    all_to_all x1 -> x0, waiting for transfers between devices: 4.07 us -> none  [on_device(): group = lax.all_to_all(group, ('y', 'c'), 0, 0, tiled=True)]
    ppermute x23 -> x27, waiting for transfers between devices: 21.9 us -> 23.7 us  [shift(): return lax.ppermute(array, axis, pairs)]
  transfers between devices with their start and end apart: 24 -> 27, of which waited for: 11 -> 13; matrix products, arithmetic and copies ran while one was open for 0% -> 0% of each run, Pallas kernels for 14% -> 15%
where the time goes in v1:
time: 105 us
  starting transfers between devices  43.2 us (41%)
  waiting for transfers between devices  23.7 us (23%)
  Pallas kernels  20.8 us (20%)
  blocking collectives  15.1 us (14%)
  between operations  1.65 us (2%)
    ppermute x27, starting transfers between devices, shift(): return lax.ppermute(array, axis, pairs)  43.2 us
    ppermute x27, waiting for transfers between devices, shift(): return lax.ppermute(array, axis, pairs)  23.7 us
    all_to_all x1, blocking collectives, on_device(): everyone = lax.all_to_all(message, ('z', 'x'), 0, 0, tiled=True)  15.1 us
    pallas_call x5, Pallas kernels, score(): pl.pallas_call(kernel, out_shape=jax.ShapeDtypeStruct((len(chunks), 8, LA...  13.1 us
    pallas_call x1, Pallas kernels, on_device(): pl.pallas_call(stage_kernel, out_shape=tuple((pltpu.VMEM(weight.shape, BF...  2.88 us
  transfers between devices with their start and end apart: 27, of which 13 were waited for; matrix products, arithmetic and copies ran while one was open for 0% of the time, Pallas kernels for 15%

profile of v1, /device:TPU:1, one launch (start us, length us, event | category | flops | bytes accessed | tf_op | source)
XLA Modules:
  0.0 104.6 jit_solution(5218542764161578390)
XLA Ops:
  0.6 2.2 %collective-permute-start.13 = (bf16[512,1024]{1,0:T(8,128)(2,1)}, bf16[512,1024]{1,0:T(8,128)(2,1)S(1)}, u32[]{:S(2)}, u32[]{:S(2)}) collective-permute-start(bf16[512,1024]{1,0:T(8,128)(2,1)} %refs_0_.2), channel_id=1, source_target_pairs={{0,8},{8,16},{16,24},{24,0},{1,9},{9,17},{17,25},{25,1},{2,10},{10... | collective-permute-start | bytes 3145736 | tf_op jit(solution)/shard_map/ppermute | solution.py:33
  2.8 1.5 %collective-permute-start.14 = (bf16[512,1024]{1,0:T(8,128)(2,1)}, bf16[512,1024]{1,0:T(8,128)(2,1)S(1)}, u32[]{:S(2)}, u32[]{:S(2)}) collective-permute-start(bf16[512,1024]{1,0:T(8,128)(2,1)} %refs_0_.2), channel_id=1, source_target_pairs={{0,24},{8,0},{16,8},{24,16},{1,25},{9,1},{17,9},{25,17},{2,26},{10... | collective-permute-start | bytes 3145736 | tf_op jit(solution)/shard_map/ppermute | solution.py:33
  4.4 1.2 %shard_map.113 = (bf16[40,1024]{1,0:T(8,128)(2,1)S(1)}, bf16[32,1024]{1,0:T(8,128)(2,1)S(1)}) custom-call(s32[2]{0:T(128)} %lengths_ref.1, s32[2,24]{1,0:T(2,128)} %tokens_ref.1, bf16[2,24,1024]{2,1,0:T(8,128)(2,1)} %hidden_ref.1, f32[1,1024]{1,0:T(1,128)} %bitcast.3), custom_call_target="tpu_custom_call" | custom-call | flops 4000000 | tf_op jit(solution)/shard_map/pallas_call | solution.py:294
  5.5 2.6 %collective-permute-start = (bf16[40,1024]{1,0:T(8,128)(2,1)S(1)}, bf16[40,1024]{1,0:T(8,128)(2,1)S(1)}, u32[]{:S(2)}, u32[]{:S(2)}) collective-permute-start(bf16[40,1024]{1,0:T(8,128)(2,1)S(1)} %get-tuple-element.34.refs_0_), channel_id=1, source_target_pairs={{0,3},{1,0},{2,1},{3,2},{4,7},{5,4},{6,5},{7,6},{8,11},{9,8},{10,9... | collective-permute-start | bytes 245768 | tf_op jit(solution)/shard_map/ppermute | solution.py:33
  8.1 0.5 collective-permute-start.1
  8.6 0.6 collective-permute-start.2
  9.2 2.9 %shard_map.114 = (bf16[1024,1024]{1,0:T(8,128)(2,1)S(1)}, bf16[1024,1024]{1,0:T(8,128)(2,1)S(1)}, bf16[1024,1024]{1,0:T(8,128)(2,1)S(1)}) custom-call(bf16[1024,1024]{1,0:T(8,128)(2,1)} %refs_0_.1, bf16[1024,1024]{1,0:T(8,128)(2,1)} %refs_1_, bf16[1024,1024]{1,0:T(8,128)(2,1)} %refs_2_), custom_call_target="tpu_custom_call" | custom-call | flops 3000000 | bytes 6300000 | tf_op jit(solution)/shard_map/pallas_call | solution.py:306
  12.1 0.0 collective-permute-done.refs_1_
  12.1 0.8 collective-permute-done.1.refs_2_
  12.9 1.1 %collective-permute-done.2.refs_3_ = bf16[40,1024]{1,0:T(8,128)(2,1)S(1)} collective-permute-done((bf16[40,1024]{1,0:T(8,128)(2,1)S(1)}, bf16[40,1024]{1,0:T(8,128)(2,1)S(1)}, u32[]{:S(2)}, u32[]{:S(2)}) %collective-permute-start.2) | collective-permute-done | bytes 81952 | tf_op jit(solution)/shard_map/ppermute | solution.py:33
  14.1 1.1 %shard_map.115 = (f32[32,1024]{1,0:T(8,128)S(1)}, bf16[32,1024]{1,0:T(8,128)(2,1)S(1)}, bf16[32,1024]{1,0:T(8,128)(2,1)S(1)}, bf16[32,1024]{1,0:T(8,128)(2,1)S(1)}, bf16[8,1024]{1,0:T(8,128)(2,1)S(1)}) custom-call(bf16[40,1024]{1,0:T(8,128)(2,1)S(1)} %get-tuple-element.34.refs_0_, bf16[40,1024]{1,0:T(8,128)(2,1)S(1)} %collective-permute-done.refs_1_, ...), custom_call_target="tpu_custom_call" | custom-call | flops 800000000 | bytes 6300000 | tf_op jit(solution)/shard_map/pallas_call | solution.py:317
  15.2 0.1 collective-permute-start.3
  15.3 1.5 %collective-permute-start.4 = (bf16[32,1024]{1,0:T(8,128)(2,1)S(1)}, bf16[32,1024]{1,0:T(8,128)(2,1)S(1)}, u32[]{:S(2)}, u32[]{:S(2)}) collective-permute-start(bf16[32,1024]{1,0:T(8,128)(2,1)S(1)} %get-tuple-element.43), channel_id=1, source_target_pairs={{0,2},{1,3},{2,0},{3,1},{4,6},{5,7},{6,4},{7,5},{8,10},{9,11},{10,... | collective-permute-start | bytes 196616 | tf_op jit(solution)/shard_map/ppermute | solution.py:33
  16.7 1.2 %collective-permute-start.5 = (bf16[32,1024]{1,0:T(8,128)(2,1)S(1)}, bf16[32,1024]{1,0:T(8,128)(2,1)S(1)}, u32[]{:S(2)}, u32[]{:S(2)}) collective-permute-start(bf16[32,1024]{1,0:T(8,128)(2,1)S(1)} %get-tuple-element.44), channel_id=1, source_target_pairs={{0,3},{1,0},{2,1},{3,2},{4,7},{5,4},{6,5},{7,6},{8,11},{9,8},{10,9... | collective-permute-start | bytes 196616 | tf_op jit(solution)/shard_map/ppermute | solution.py:33
  17.9 2.6 %collective-permute-done.3.first_ref = bf16[32,1024]{1,0:T(8,128)(2,1)S(1)} collective-permute-done((bf16[32,1024]{1,0:T(8,128)(2,1)S(1)}, bf16[32,1024]{1,0:T(8,128)(2,1)S(1)}, u32[]{:S(2)}, u32[]{:S(2)}) %collective-permute-start.3) | collective-permute-done | bytes 65568 | tf_op jit(solution)/shard_map/ppermute | solution.py:33
  20.6 0.0 collective-permute-done.4.second_ref
  20.6 0.6 collective-permute-done.5.third_ref
  21.2 0.1 shard_map.116.refs_0_
  21.3 2.2 %collective-permute-start.6 = (bf16[32,1024]{1,0:T(8,128)(2,1)S(1)}, bf16[32,1024]{1,0:T(8,128)(2,1)S(1)}, u32[]{:S(2)}, u32[]{:S(2)}) collective-permute-start(bf16[32,1024]{1,0:T(8,128)(2,1)S(1)} %shard_map.116.refs_0_), channel_id=1, source_target_pairs={{0,3},{1,0},{2,1},{3,2},{4,7},{5,4},{6,5},{7,6},{8,11},{9,8},{10,9... | collective-permute-start | bytes 196616 | tf_op jit(solution)/shard_map/ppermute | solution.py:33
  23.5 0.4 collective-permute-start.7
  23.9 0.2 collective-permute-start.8
  24.2 0.7 collective-permute-done.6.refs_1_
  24.8 3.3 %collective-permute-done.7.refs_2_ = bf16[32,1024]{1,0:T(8,128)(2,1)S(1)} collective-permute-done((bf16[32,1024]{1,0:T(8,128)(2,1)S(1)}, bf16[32,1024]{1,0:T(8,128)(2,1)S(1)}, u32[]{:S(2)}, u32[]{:S(2)}) %collective-permute-start.7) | collective-permute-done | bytes 65568 | tf_op jit(solution)/shard_map/ppermute | solution.py:33
  28.2 0.6 collective-permute-done.8.refs_3_
  28.8 0.0 collective-permute-done.13.refs_1_
  28.8 0.0 collective-permute-done.14.refs_2_
  28.9 0.2 shard_map.118.refs_2_.refs_3_
  29.1 5.2 %collective-permute-start.15 = (bf16[1536,1024]{1,0:T(8,128)(2,1)S(1)}, bf16[1536,1024]{1,0:T(8,128)(2,1)S(1)}, u32[]{:S(2)}, u32[]{:S(2)}) collective-permute-start(bf16[1536,1024]{1,0:T(8,128)(2,1)S(1)} %shard_map.118.refs_2_.refs_3_), channel_id=1, source_target_pairs={{0,4},{4,0},{1,5},{5,1},{2,6},{6,2},{3,7},{7,3},{8,12},{12,8},{9,1... | collective-permute-start | bytes 9437192 | tf_op jit(solution)/shard_map/ppermute | solution.py:33
  34.3 1.6 %collective-permute-start.9 = (bf16[136,1024]{1,0:T(8,128)(2,1)S(1)}, bf16[136,1024]{1,0:T(8,128)(2,1)S(1)}, u32[]{:S(2)}, u32[]{:S(2)}) collective-permute-start(bf16[136,1024]{1,0:T(8,128)(2,1)S(1)} %shard_map.117.refs_0_), channel_id=1, source_target_pairs={{0,32},{32,64},{64,96},{96,128},{128,160},{160,192},{192,224},{224... | collective-permute-start | bytes 835592 | tf_op jit(solution)/shard_map/ppermute | solution.py:33
  35.9 4.0 %collective-permute-start.11 = (bf16[136,1024]{1,0:T(8,128)(2,1)S(1)}, bf16[136,1024]{1,0:T(8,128)(2,1)S(1)}, u32[]{:S(2)}, u32[]{:S(2)}) collective-permute-start(bf16[136,1024]{1,0:T(8,128)(2,1)S(1)} %shard_map.117.refs_0_), channel_id=1, source_target_pairs={{0,224},{32,0},{64,32},{96,64},{128,96},{160,128},{192,160},{224,1... | collective-permute-start | bytes 835592 | tf_op jit(solution)/shard_map/ppermute | solution.py:33
  39.9 0.5 collective-permute-start.18
  40.4 2.2 %collective-permute-start.19 = (bf16[256,1024]{1,0:T(8,128)(2,1)S(1)}, bf16[256,1024]{1,0:T(8,128)(2,1)S(1)}, u32[]{:S(2)}, u32[]{:S(2)}) collective-permute-start(bf16[256,1024]{1,0:T(8,128)(2,1)S(1)} %slice.13), channel_id=1, source_target_pairs={{0,24},{8,0},{16,8},{24,16},{1,25},{9,1},{17,9},{25,17},{2,26},{10... | collective-permute-start | bytes 1572872 | tf_op jit(solution)/shard_map/ppermute | solution.py:33
  42.7 4.1 %collective-permute-done.9.refs_0_ = bf16[136,1024]{1,0:T(8,128)(2,1)S(1)} collective-permute-done((bf16[136,1024]{1,0:T(8,128)(2,1)S(1)}, bf16[136,1024]{1,0:T(8,128)(2,1)S(1)}, u32[]{:S(2)}, u32[]{:S(2)}) %collective-permute-start.9) | collective-permute-done | bytes 278560 | tf_op jit(solution)/shard_map/ppermute | solution.py:33
  46.8 0.0 collective-permute-start.10
  46.8 0.0 collective-permute-done.11.refs_1_
  46.8 2.7 %collective-permute-start.12 = (bf16[136,1024]{1,0:T(8,128)(2,1)S(1)}, bf16[136,1024]{1,0:T(8,128)(2,1)S(1)}, u32[]{:S(2)}, u32[]{:S(2)}) collective-permute-start(bf16[136,1024]{1,0:T(8,128)(2,1)S(1)} %collective-permute-done.11.refs_1_), channel_id=1, source_target_pairs={{0,224},{32,0},{64,32},{96,64},{128,96},{160,128},{192,160},{224,1... | collective-permute-start | bytes 835592 | tf_op jit(solution)/shard_map/ppermute | solution.py:33
  49.5 2.4 %shard_map.119.near_ref = f32[2,8,128]{2,1,0:T(8,128)S(1)} custom-call(bf16[136,1024]{1,0:T(8,128)(2,1)S(1)} %collective-permute-done.9.refs_0_, bf16[136,1024]{1,0:T(8,128)(2,1)S(1)} %collective-permute-done.11.refs_1_, bf16[1536,1024]{1,0:T(8,128)(2,1)S(1)} %shard_map.118.refs_2_.refs_3_, bf16[1536,1024]{1,0:T(8,128)(2,1)S(1)} %collective-permute-done.15.refs_3_.refs_4_), custom_call_target="tpu_custom_call" | custom-call | flops 1610612736 | bytes 6291456 | tf_op jit(solution)/shard_map/pallas_call | solution.py:375
  51.9 3.7 %collective-permute-done.10.refs_0_.refs_2_ = bf16[136,1024]{1,0:T(8,128)(2,1)S(1)} collective-permute-done((bf16[136,1024]{1,0:T(8,128)(2,1)S(1)}, bf16[136,1024]{1,0:T(8,128)(2,1)S(1)}, u32[]{:S(2)}, u32[]{:S(2)}) %collective-permute-start.10) | collective-permute-done | bytes 278560 | tf_op jit(solution)/shard_map/ppermute | solution.py:33
  55.5 0.0 collective-permute-done.12.refs_1_.refs_3_
  55.5 0.0 collective-permute-done.18.refs_0_
  55.6 0.0 collective-permute-done.19.refs_1_
  55.6 0.1 shard_map.121.refs_4_.refs_5_
  55.6 1.6 %collective-permute-start.20 = (bf16[512,1024]{1,0:T(8,128)(2,1)S(1)}, bf16[512,1024]{1,0:T(8,128)(2,1)S(1)}, u32[]{:S(2)}, u32[]{:S(2)}) collective-permute-start(bf16[512,1024]{1,0:T(8,128)(2,1)S(1)} %shard_map.121.refs_4_.refs_5_), channel_id=1, source_target_pairs={{0,4},{4,0},{1,5},{5,1},{2,6},{6,2},{3,7},{7,3},{8,12},{12,8},{9,1... | collective-permute-start | bytes 3145736 | tf_op jit(solution)/shard_map/ppermute | solution.py:33
  57.3 2.7 %collective-permute-start.17 = (bf16[136,1024]{1,0:T(8,128)(2,1)S(1)}, bf16[136,1024]{1,0:T(8,128)(2,1)S(1)}, u32[]{:S(2)}, u32[]{:S(2)}) collective-permute-start(bf16[136,1024]{1,0:T(8,128)(2,1)S(1)} %collective-permute-done.12.refs_1_.refs_3_), channel_id=1, source_target_pairs={{0,224},{32,0},{64,32},{96,64},{128,96},{160,128},{192,160},{224,1... | collective-permute-start | bytes 835592 | tf_op jit(solution)/shard_map/ppermute | solution.py:33
  59.9 2.4 %shard_map.120.middle_ref = f32[2,8,128]{2,1,0:T(8,128)S(1)} custom-call(bf16[136,1024]{1,0:T(8,128)(2,1)S(1)} %collective-permute-done.10.refs_0_.refs_2_, bf16[136,1024]{1,0:T(8,128)(2,1)S(1)} %collective-permute-done.12.refs_1_.refs_3_, bf16[1536,1024]{1,0:T(8,128)(2,1)S(1)} %shard_map.118.refs_2_.refs_3_, ...), custom_call_target="tpu_custom_call" | custom-call | flops 1610612736 | bytes 6291456 | tf_op jit(solution)/shard_map/pallas_call | solution.py:375
  62.3 2.0 %shard_map.122.far_ref = f32[4,8,128]{2,1,0:T(8,128)S(1)} custom-call(bf16[136,1024]{1,0:T(8,128)(2,1)S(1)} %collective-permute-done.9.refs_0_, bf16[136,1024]{1,0:T(8,128)(2,1)S(1)} %collective-permute-done.11.refs_1_, bf16[136,1024]{1,0:T(8,128)(2,1)S(1)} %collective-permute-done.10.refs_0_.refs_2_, ...), custom_call_target="tpu_custom_call" | custom-call | flops 1073741824 | bytes 2097152 | tf_op jit(solution)/shard_map/pallas_call | solution.py:375
  64.4 2.2 %collective-permute-done.16.refs_0_ = bf16[136,1024]{1,0:T(8,128)(2,1)S(1)} collective-permute-done((bf16[136,1024]{1,0:T(8,128)(2,1)S(1)}, bf16[136,1024]{1,0:T(8,128)(2,1)S(1)}, u32[]{:S(2)}, u32[]{:S(2)}) %collective-permute-start.16) | collective-permute-done | bytes 278560 | tf_op jit(solution)/shard_map/ppermute | solution.py:33
  66.6 0.0 collective-permute-done.17.refs_1_
  66.6 2.0 %collective-permute-start.21 = (bf16[136,512]{1,0:T(8,128)(2,1)S(1)}, bf16[136,512]{1,0:T(8,128)(2,1)S(1)}, u32[]{:S(2)}, u32[]{:S(2)}) collective-permute-start(bf16[136,512]{1,0:T(8,128)(2,1)S(1)} %slice.14), channel_id=1, source_target_pairs={{0,32},{32,64},{64,96},{96,128},{128,160},{160,192},{192,224},{224... | collective-permute-start | bytes 417800 | tf_op jit(solution)/shard_map/ppermute | solution.py:33
  68.6 1.1 %collective-permute-start.22 = (bf16[136,512]{1,0:T(8,128)(2,1)S(1)}, bf16[136,512]{1,0:T(8,128)(2,1)S(1)}, u32[]{:S(2)}, u32[]{:S(2)}) collective-permute-start(bf16[136,512]{1,0:T(8,128)(2,1)S(1)} %slice.15), channel_id=1, source_target_pairs={{0,224},{32,0},{64,32},{96,64},{128,96},{160,128},{192,160},{224,1... | collective-permute-start | bytes 417800 | tf_op jit(solution)/shard_map/ppermute | solution.py:33
  69.7 3.1 %shard_map.123.outer_ref = f32[2,8,128]{2,1,0:T(8,128)S(1)} custom-call(bf16[136,1024]{1,0:T(8,128)(2,1)S(1)} %collective-permute-done.16.refs_0_, bf16[136,1024]{1,0:T(8,128)(2,1)S(1)} %collective-permute-done.17.refs_1_, bf16[1536,1024]{1,0:T(8,128)(2,1)S(1)} %shard_map.118.refs_2_.refs_3_, bf16[1536,1024]{1,0:T(8,128)(2,1)S(1)} %collective-permute-done.15.refs_3_.refs_4_, ...), custom_call_target="tpu_custom_call" | custom-call | flops 2147483648 | bytes 8388608 | tf_op jit(solution)/shard_map/pallas_call | solution.py:375
  72.8 0.3 collective-permute-done.22.refs_2_
  73.1 3.1 %shard_map.124.last_ref = f32[2,8,128]{2,1,0:T(8,128)S(1)} custom-call(bf16[136,1024]{1,0:T(8,128)(2,1)S(1)} %shard_map.117.refs_0_, bf16[136,512]{1,0:T(8,128)(2,1)S(1)} %collective-permute-done.21.refs_1_, bf16[136,512]{1,0:T(8,128)(2,1)S(1)} %collective-permute-done.22.refs_2_, bf16[1536,1024]{1,0:T(8,128)(2,1)S(1)} %shard_map.118.refs_2_.refs_3_, ...), custom_call_target="tpu_custom_call" | custom-call | flops 2147483648 | bytes 8388608 | tf_op jit(solution)/shard_map/pallas_call | solution.py:375
  76.2 0.3 shard_map.125
  76.5 15.1 %all_to_all.5.everyone_ref = f32[32,8,128]{2,1,0:T(8,128)S(1)} all-to-all(f32[32,8,128]{2,1,0:T(8,128)S(1)} %get-tuple-element.64), channel_id=1, replica_groups=mesh['z'=8,'y'=4,'c'=2,'x'=4] {'z','x'}, dimensions={0} | all-to-all | bytes 262144 | tf_op jit(solution)/shard_map/all_to_all | solution.py:417
  91.7 0.3 shard_map.126
  92.0 3.4 %collective-permute-start.23 = (f32[8,128]{1,0:T(8,128)S(1)}, f32[8,128]{1,0:T(8,128)S(1)}, u32[]{:S(2)}, u32[]{:S(2)}) collective-permute-start(f32[8,128]{1,0:T(8,128)S(1)} %shard_map.126), channel_id=1, source_target_pairs={{0,4},{4,0},{1,5},{5,1},{2,6},{6,2},{3,7},{7,3},{8,12},{12,8},{9,1... | collective-permute-start | bytes 12296 | tf_op jit(solution)/shard_map/ppermute | solution.py:33
  95.4 0.8 collective-permute-done.23
  96.2 0.1 collective-permute-start.24
  96.3 2.5 %collective-permute-start.25 = (f32[16,128]{1,0:T(8,128)S(1)}, f32[16,128]{1,0:T(8,128)S(1)}, u32[]{:S(2)}, u32[]{:S(2)}) collective-permute-start(f32[16,128]{1,0:T(8,128)S(1)} %pad_maximum_fusion.refs_0_), channel_id=1, source_target_pairs={{0,24},{8,0},{16,8},{24,16},{1,25},{9,1},{17,9},{25,17},{2,26},{10... | collective-permute-start | bytes 24584 | tf_op jit(solution)/shard_map/ppermute | solution.py:33
  98.9 0.5 collective-permute-start.26
  100.1 0.0 collective-permute-done.24.refs_1_
  100.1 2.8 %collective-permute-done.26.refs_3_ = f32[16,128]{1,0:T(8,128)S(1)} collective-permute-done((f32[16,128]{1,0:T(8,128)S(1)}, f32[16,128]{1,0:T(8,128)S(1)}, u32[]{:S(2)}, u32[]{:S(2)}) %collective-permute-start.26) | collective-permute-done | bytes 8224 | tf_op jit(solution)/shard_map/ppermute | solution.py:33
  102.9 1.5 %shard_map.127 = (f32[2]{0:T(128)}, f32[2]{0:T(128)}) custom-call(s32[1]{0:T(128)S(6)} %copy.12.cutoff_ref, f32[16,128]{1,0:T(8,128)S(1)} %pad_maximum_fusion.refs_0_, f32[16,128]{1,0:T(8,128)S(1)} %collective-permute-done.24.refs_1_, f32[16,128]{1,0:T(8,128)S(1)} %collective-permute-done.25.refs_2_, f32[16,128]{1,0:T(8,128)S(1)} %collective-permute-done.26.refs_3_), custom_call_target="tpu_custom_call" | custom-call | flops 1000000 | tf_op jit(solution)/shard_map/pallas_call | solution.py:427
  (15 shorter events, 0.1 us)
Async XLA Ops:
  0.6 28.2 %collective-permute-start.13 = (bf16[512,1024]{1,0:T(8,128)(2,1)}, bf16[512,1024]{1,0:T(8,128)(2,1)S(1)}, u32[]{:S(2)}, u32[]{:S(2)}) collective-permute-start(bf16[512,1024]{1,0:T(8,128)(2,1)} %refs_0_.2), channel_id=1, source_target_pairs={{0,8},{8,16},{16,24},{24,0},{1,9},{9,17},{17,25},{25,1},{2,10},{10... | collective-permute-start | bytes 3145736 | tf_op jit(solution)/shard_map/ppermute | solution.py:33
  2.8 26.0 %collective-permute-start.14 = (bf16[512,1024]{1,0:T(8,128)(2,1)}, bf16[512,1024]{1,0:T(8,128)(2,1)S(1)}, u32[]{:S(2)}, u32[]{:S(2)}) collective-permute-start(bf16[512,1024]{1,0:T(8,128)(2,1)} %refs_0_.2), channel_id=1, source_target_pairs={{0,24},{8,0},{16,8},{24,16},{1,25},{9,1},{17,9},{25,17},{2,26},{10... | collective-permute-start | bytes 3145736 | tf_op jit(solution)/shard_map/ppermute | solution.py:33
  5.5 6.6 %collective-permute-start = (bf16[40,1024]{1,0:T(8,128)(2,1)S(1)}, bf16[40,1024]{1,0:T(8,128)(2,1)S(1)}, u32[]{:S(2)}, u32[]{:S(2)}) collective-permute-start(bf16[40,1024]{1,0:T(8,128)(2,1)S(1)} %get-tuple-element.34.refs_0_), channel_id=1, source_target_pairs={{0,3},{1,0},{2,1},{3,2},{4,7},{5,4},{6,5},{7,6},{8,11},{9,8},{10,9... | collective-permute-start | bytes 245768 | tf_op jit(solution)/shard_map/ppermute | solution.py:33
  8.1 4.9 %collective-permute-start.1 = (bf16[40,1024]{1,0:T(8,128)(2,1)S(1)}, bf16[40,1024]{1,0:T(8,128)(2,1)S(1)}, u32[]{:S(2)}, u32[]{:S(2)}) collective-permute-start(bf16[40,1024]{1,0:T(8,128)(2,1)S(1)} %get-tuple-element.34.refs_0_), channel_id=1, source_target_pairs={{0,2},{1,3},{2,0},{3,1},{4,6},{5,7},{6,4},{7,5},{8,10},{9,11},{10,... | collective-permute-start | bytes 245768 | tf_op jit(solution)/shard_map/ppermute | solution.py:33
  8.6 5.4 %collective-permute-start.2 = (bf16[40,1024]{1,0:T(8,128)(2,1)S(1)}, bf16[40,1024]{1,0:T(8,128)(2,1)S(1)}, u32[]{:S(2)}, u32[]{:S(2)}) collective-permute-start(bf16[40,1024]{1,0:T(8,128)(2,1)S(1)} %get-tuple-element.34.refs_0_), channel_id=1, source_target_pairs={{0,1},{1,2},{2,3},{3,0},{4,5},{5,6},{6,7},{7,4},{8,9},{9,10},{10,1... | collective-permute-start | bytes 245768 | tf_op jit(solution)/shard_map/ppermute | solution.py:33
  14.1 7.1 %copy-start.1 = (f32[1024]{0:T(1024)S(1)}, f32[1024]{0:T(1024)}, u32[]{:S(2)}) copy-start(f32[1024]{0:T(1024)} %param.18) | copy-start | bytes 12292
  14.1 14.8 %copy-start = (bf16[512,1024]{1,0:T(8,128)(2,1)S(1)}, bf16[512,1024]{1,0:T(8,128)(2,1)}, u32[]{:S(2)}) copy-start(bf16[512,1024]{1,0:T(8,128)(2,1)} %refs_0_.2) | copy-start | bytes 3145732
  15.2 5.4 %collective-permute-start.3 = (bf16[32,1024]{1,0:T(8,128)(2,1)S(1)}, bf16[32,1024]{1,0:T(8,128)(2,1)S(1)}, u32[]{:S(2)}, u32[]{:S(2)}) collective-permute-start(bf16[32,1024]{1,0:T(8,128)(2,1)S(1)} %get-tuple-element.42), channel_id=1, source_target_pairs={{0,1},{1,2},{2,3},{3,0},{4,5},{5,6},{6,7},{7,4},{8,9},{9,10},{10,1... | collective-permute-start | bytes 196616 | tf_op jit(solution)/shard_map/ppermute | solution.py:33
  15.3 5.3 %collective-permute-start.4 = (bf16[32,1024]{1,0:T(8,128)(2,1)S(1)}, bf16[32,1024]{1,0:T(8,128)(2,1)S(1)}, u32[]{:S(2)}, u32[]{:S(2)}) collective-permute-start(bf16[32,1024]{1,0:T(8,128)(2,1)S(1)} %get-tuple-element.43), channel_id=1, source_target_pairs={{0,2},{1,3},{2,0},{3,1},{4,6},{5,7},{6,4},{7,5},{8,10},{9,11},{10,... | collective-permute-start | bytes 196616 | tf_op jit(solution)/shard_map/ppermute | solution.py:33
  16.7 4.4 %collective-permute-start.5 = (bf16[32,1024]{1,0:T(8,128)(2,1)S(1)}, bf16[32,1024]{1,0:T(8,128)(2,1)S(1)}, u32[]{:S(2)}, u32[]{:S(2)}) collective-permute-start(bf16[32,1024]{1,0:T(8,128)(2,1)S(1)} %get-tuple-element.44), channel_id=1, source_target_pairs={{0,3},{1,0},{2,1},{3,2},{4,7},{5,4},{6,5},{7,6},{8,11},{9,8},{10,9... | collective-permute-start | bytes 196616 | tf_op jit(solution)/shard_map/ppermute | solution.py:33
  21.3 3.5 %collective-permute-start.6 = (bf16[32,1024]{1,0:T(8,128)(2,1)S(1)}, bf16[32,1024]{1,0:T(8,128)(2,1)S(1)}, u32[]{:S(2)}, u32[]{:S(2)}) collective-permute-start(bf16[32,1024]{1,0:T(8,128)(2,1)S(1)} %shard_map.116.refs_0_), channel_id=1, source_target_pairs={{0,3},{1,0},{2,1},{3,2},{4,7},{5,4},{6,5},{7,6},{8,11},{9,8},{10,9... | collective-permute-start | bytes 196616 | tf_op jit(solution)/shard_map/ppermute | solution.py:33
  23.5 4.7 %collective-permute-start.7 = (bf16[32,1024]{1,0:T(8,128)(2,1)S(1)}, bf16[32,1024]{1,0:T(8,128)(2,1)S(1)}, u32[]{:S(2)}, u32[]{:S(2)}) collective-permute-start(bf16[32,1024]{1,0:T(8,128)(2,1)S(1)} %shard_map.116.refs_0_), channel_id=1, source_target_pairs={{0,2},{1,3},{2,0},{3,1},{4,6},{5,7},{6,4},{7,5},{8,10},{9,11},{10,... | collective-permute-start | bytes 196616 | tf_op jit(solution)/shard_map/ppermute | solution.py:33
  23.9 4.9 %collective-permute-start.8 = (bf16[32,1024]{1,0:T(8,128)(2,1)S(1)}, bf16[32,1024]{1,0:T(8,128)(2,1)S(1)}, u32[]{:S(2)}, u32[]{:S(2)}) collective-permute-start(bf16[32,1024]{1,0:T(8,128)(2,1)S(1)} %shard_map.116.refs_0_), channel_id=1, source_target_pairs={{0,1},{1,2},{2,3},{3,0},{4,5},{5,6},{6,7},{7,4},{8,9},{9,10},{10,1... | collective-permute-start | bytes 196616 | tf_op jit(solution)/shard_map/ppermute | solution.py:33
  29.1 20.4 %collective-permute-start.15 = (bf16[1536,1024]{1,0:T(8,128)(2,1)S(1)}, bf16[1536,1024]{1,0:T(8,128)(2,1)S(1)}, u32[]{:S(2)}, u32[]{:S(2)}) collective-permute-start(bf16[1536,1024]{1,0:T(8,128)(2,1)S(1)} %shard_map.118.refs_2_.refs_3_), channel_id=1, source_target_pairs={{0,4},{4,0},{1,5},{5,1},{2,6},{6,2},{3,7},{7,3},{8,12},{12,8},{9,1... | collective-permute-start | bytes 9437192 | tf_op jit(solution)/shard_map/ppermute | solution.py:33
  34.3 12.5 %collective-permute-start.9 = (bf16[136,1024]{1,0:T(8,128)(2,1)S(1)}, bf16[136,1024]{1,0:T(8,128)(2,1)S(1)}, u32[]{:S(2)}, u32[]{:S(2)}) collective-permute-start(bf16[136,1024]{1,0:T(8,128)(2,1)S(1)} %shard_map.117.refs_0_), channel_id=1, source_target_pairs={{0,32},{32,64},{64,96},{96,128},{128,160},{160,192},{192,224},{224... | collective-permute-start | bytes 835592 | tf_op jit(solution)/shard_map/ppermute | solution.py:33
  35.9 10.9 %collective-permute-start.11 = (bf16[136,1024]{1,0:T(8,128)(2,1)S(1)}, bf16[136,1024]{1,0:T(8,128)(2,1)S(1)}, u32[]{:S(2)}, u32[]{:S(2)}) collective-permute-start(bf16[136,1024]{1,0:T(8,128)(2,1)S(1)} %shard_map.117.refs_0_), channel_id=1, source_target_pairs={{0,224},{32,0},{64,32},{96,64},{128,96},{160,128},{192,160},{224,1... | collective-permute-start | bytes 835592 | tf_op jit(solution)/shard_map/ppermute | solution.py:33
  39.9 15.6 %collective-permute-start.18 = (bf16[256,1024]{1,0:T(8,128)(2,1)S(1)}, bf16[256,1024]{1,0:T(8,128)(2,1)S(1)}, u32[]{:S(2)}, u32[]{:S(2)}) collective-permute-start(bf16[256,1024]{1,0:T(8,128)(2,1)S(1)} %slice.12), channel_id=1, source_target_pairs={{0,8},{8,16},{16,24},{24,0},{1,9},{9,17},{17,25},{25,1},{2,10},{10... | collective-permute-start | bytes 1572872 | tf_op jit(solution)/shard_map/ppermute | solution.py:33
  40.4 15.1 %collective-permute-start.19 = (bf16[256,1024]{1,0:T(8,128)(2,1)S(1)}, bf16[256,1024]{1,0:T(8,128)(2,1)S(1)}, u32[]{:S(2)}, u32[]{:S(2)}) collective-permute-start(bf16[256,1024]{1,0:T(8,128)(2,1)S(1)} %slice.13), channel_id=1, source_target_pairs={{0,24},{8,0},{16,8},{24,16},{1,25},{9,1},{17,9},{25,17},{2,26},{10... | collective-permute-start | bytes 1572872 | tf_op jit(solution)/shard_map/ppermute | solution.py:33
  46.8 8.8 %collective-permute-start.10 = (bf16[136,1024]{1,0:T(8,128)(2,1)S(1)}, bf16[136,1024]{1,0:T(8,128)(2,1)S(1)}, u32[]{:S(2)}, u32[]{:S(2)}) collective-permute-start(bf16[136,1024]{1,0:T(8,128)(2,1)S(1)} %collective-permute-done.9.refs_0_), channel_id=1, source_target_pairs={{0,32},{32,64},{64,96},{96,128},{128,160},{160,192},{192,224},{224... | collective-permute-start | bytes 835592 | tf_op jit(solution)/shard_map/ppermute | solution.py:33
  46.8 8.8 %collective-permute-start.12 = (bf16[136,1024]{1,0:T(8,128)(2,1)S(1)}, bf16[136,1024]{1,0:T(8,128)(2,1)S(1)}, u32[]{:S(2)}, u32[]{:S(2)}) collective-permute-start(bf16[136,1024]{1,0:T(8,128)(2,1)S(1)} %collective-permute-done.11.refs_1_), channel_id=1, source_target_pairs={{0,224},{32,0},{64,32},{96,64},{128,96},{160,128},{192,160},{224,1... | collective-permute-start | bytes 835592 | tf_op jit(solution)/shard_map/ppermute | solution.py:33
  55.6 6.7 %collective-permute-start.20 = (bf16[512,1024]{1,0:T(8,128)(2,1)S(1)}, bf16[512,1024]{1,0:T(8,128)(2,1)S(1)}, u32[]{:S(2)}, u32[]{:S(2)}) collective-permute-start(bf16[512,1024]{1,0:T(8,128)(2,1)S(1)} %shard_map.121.refs_4_.refs_5_), channel_id=1, source_target_pairs={{0,4},{4,0},{1,5},{5,1},{2,6},{6,2},{3,7},{7,3},{8,12},{12,8},{9,1... | collective-permute-start | bytes 3145736 | tf_op jit(solution)/shard_map/ppermute | solution.py:33
  57.2 9.3 %collective-permute-start.16 = (bf16[136,1024]{1,0:T(8,128)(2,1)S(1)}, bf16[136,1024]{1,0:T(8,128)(2,1)S(1)}, u32[]{:S(2)}, u32[]{:S(2)}) collective-permute-start(bf16[136,1024]{1,0:T(8,128)(2,1)S(1)} %collective-permute-done.10.refs_0_.refs_2_), channel_id=1, source_target_pairs={{0,32},{32,64},{64,96},{96,128},{128,160},{160,192},{192,224},{224... | collective-permute-start | bytes 835592 | tf_op jit(solution)/shard_map/ppermute | solution.py:33
  57.3 9.3 %collective-permute-start.17 = (bf16[136,1024]{1,0:T(8,128)(2,1)S(1)}, bf16[136,1024]{1,0:T(8,128)(2,1)S(1)}, u32[]{:S(2)}, u32[]{:S(2)}) collective-permute-start(bf16[136,1024]{1,0:T(8,128)(2,1)S(1)} %collective-permute-done.12.refs_1_.refs_3_), channel_id=1, source_target_pairs={{0,224},{32,0},{64,32},{96,64},{128,96},{160,128},{192,160},{224,1... | collective-permute-start | bytes 835592 | tf_op jit(solution)/shard_map/ppermute | solution.py:33
  66.6 6.2 %collective-permute-start.21 = (bf16[136,512]{1,0:T(8,128)(2,1)S(1)}, bf16[136,512]{1,0:T(8,128)(2,1)S(1)}, u32[]{:S(2)}, u32[]{:S(2)}) collective-permute-start(bf16[136,512]{1,0:T(8,128)(2,1)S(1)} %slice.14), channel_id=1, source_target_pairs={{0,32},{32,64},{64,96},{96,128},{128,160},{160,192},{192,224},{224... | collective-permute-start | bytes 417800 | tf_op jit(solution)/shard_map/ppermute | solution.py:33
  68.6 4.5 %collective-permute-start.22 = (bf16[136,512]{1,0:T(8,128)(2,1)S(1)}, bf16[136,512]{1,0:T(8,128)(2,1)S(1)}, u32[]{:S(2)}, u32[]{:S(2)}) collective-permute-start(bf16[136,512]{1,0:T(8,128)(2,1)S(1)} %slice.15), channel_id=1, source_target_pairs={{0,224},{32,0},{64,32},{96,64},{128,96},{160,128},{192,160},{224,1... | collective-permute-start | bytes 417800 | tf_op jit(solution)/shard_map/ppermute | solution.py:33
  92.0 4.2 %collective-permute-start.23 = (f32[8,128]{1,0:T(8,128)S(1)}, f32[8,128]{1,0:T(8,128)S(1)}, u32[]{:S(2)}, u32[]{:S(2)}) collective-permute-start(f32[8,128]{1,0:T(8,128)S(1)} %shard_map.126), channel_id=1, source_target_pairs={{0,4},{4,0},{1,5},{5,1},{2,6},{6,2},{3,7},{7,3},{8,12},{12,8},{9,1... | collective-permute-start | bytes 12296 | tf_op jit(solution)/shard_map/ppermute | solution.py:33
  96.2 3.9 %collective-permute-start.24 = (f32[16,128]{1,0:T(8,128)S(1)}, f32[16,128]{1,0:T(8,128)S(1)}, u32[]{:S(2)}, u32[]{:S(2)}) collective-permute-start(f32[16,128]{1,0:T(8,128)S(1)} %pad_maximum_fusion.refs_0_), channel_id=1, source_target_pairs={{0,8},{8,16},{16,24},{24,0},{1,9},{9,17},{17,25},{25,1},{2,10},{10... | collective-permute-start | bytes 24584 | tf_op jit(solution)/shard_map/ppermute | solution.py:33
  96.3 3.7 %collective-permute-start.25 = (f32[16,128]{1,0:T(8,128)S(1)}, f32[16,128]{1,0:T(8,128)S(1)}, u32[]{:S(2)}, u32[]{:S(2)}) collective-permute-start(f32[16,128]{1,0:T(8,128)S(1)} %pad_maximum_fusion.refs_0_), channel_id=1, source_target_pairs={{0,24},{8,0},{16,8},{24,16},{1,25},{9,1},{17,9},{25,17},{2,26},{10... | collective-permute-start | bytes 24584 | tf_op jit(solution)/shard_map/ppermute | solution.py:33
  98.9 4.0 %collective-permute-start.26 = (f32[16,128]{1,0:T(8,128)S(1)}, f32[16,128]{1,0:T(8,128)S(1)}, u32[]{:S(2)}, u32[]{:S(2)}) collective-permute-start(f32[16,128]{1,0:T(8,128)S(1)} %pad_maximum_fusion.refs_0_), channel_id=1, source_target_pairs={{0,16},{8,24},{16,0},{24,8},{1,17},{9,25},{17,1},{25,9},{2,18},{10... | collective-permute-start | bytes 24584 | tf_op jit(solution)/shard_map/ppermute | solution.py:33
